TPU v7x, 128 devices: a whole 4x4x4 slice. The times are simulated.
128 devices in a mesh: data: 128 (over z, y, x, core).
Axes of the slice: x: 4, y: 4, z: 4, core: 2. Of those that a mesh axis runs over, the one named last changes fastest.
Arguments:
- q_in: bfloat16 [8192, 512], P('data')
- d_in: bfloat16 [2, 8192, 512], P(None, 'data')
- temperature: float32 [], replicated
- q_w1: bfloat16 [2, 512, 2048], replicated
- q_w2: bfloat16 [2, 2048, 512], replicated
- q_proj: bfloat16 [512, 512], replicated
- d_w1: bfloat16 [2, 512, 2048], replicated
- d_w2: bfloat16 [2, 2048, 512], replicated
- d_proj: bfloat16 [512, 512], replicated
Outputs:
- output 1: float32 [], replicated
- output 2: float32 [2, 512, 2048], replicated
- output 3: float32 [2, 2048, 512], replicated
- output 4: float32 [512, 512], replicated
- output 5: float32 [2, 512, 2048], replicated
- output 6: float32 [2, 2048, 512], replicated
- output 7: float32 [512, 512], replicated
All inputs are finite; a program needn't handle non-finite values.
Results may differ from a plain program's by a relative error of at most 0.00628917.
Values are sent between devices in bfloat16 or wider.
A program may use at most 1 GiB of HBM per device.

v0:
```python
import jax
import jax.numpy as jnp
from jax import lax
from jax.sharding import PartitionSpec as P

SUB_COUNT = 4
ROWS_CONTRACT = (((0,), (0,)), ((), ()))
LAST_CONTRACT = (((1,), (1,)), ((), ()))


def tower_forward(row_block, w_one, w_two, w_proj):
    hidden = row_block
    saved = []
    for layer in range(2):
        pre_act = jnp.dot(hidden, w_one[layer], preferred_element_type=jnp.float32)
        act_bf = jax.nn.gelu(pre_act).astype(jnp.bfloat16)
        saved.append((hidden, pre_act, act_bf))
        hidden = (hidden.astype(jnp.float32) + jnp.dot(act_bf, w_two[layer], preferred_element_type=jnp.float32)).astype(jnp.bfloat16)
    out_reps = jnp.dot(hidden, w_proj, preferred_element_type=jnp.float32).astype(jnp.bfloat16)
    return out_reps, hidden, saved


def tower_backward(upstream, w_one, w_two, w_proj, hidden, saved):
    g_proj = lax.dot_general(hidden, upstream, ROWS_CONTRACT, preferred_element_type=jnp.float32)
    resid_grad = lax.dot_general(upstream, w_proj, LAST_CONTRACT, preferred_element_type=jnp.float32)
    grads_one = [None, None]
    grads_two = [None, None]
    for layer in (1, 0):
        h_in, pre_act, act_bf = saved[layer]
        resid_bf = resid_grad.astype(jnp.bfloat16)
        grads_two[layer] = lax.dot_general(act_bf, resid_bf, ROWS_CONTRACT, preferred_element_type=jnp.float32)
        act_grad = lax.dot_general(resid_bf, w_two[layer], LAST_CONTRACT, preferred_element_type=jnp.float32)
        gelu_back = jax.vjp(jax.nn.gelu, pre_act)[1]
        pre_grad = gelu_back(act_grad)[0].astype(jnp.bfloat16)
        grads_one[layer] = lax.dot_general(h_in, pre_grad, ROWS_CONTRACT, preferred_element_type=jnp.float32)
        if layer == 1:
            resid_grad = resid_grad + lax.dot_general(pre_grad, w_one[layer], LAST_CONTRACT, preferred_element_type=jnp.float32)
    return jnp.stack(grads_one), jnp.stack(grads_two), g_proj


def tower_grads(row_subs, up_subs, w_one, w_two, w_proj):
    def body(running, block_in):
        row_block, upstream = block_in
        hidden, saved = tower_forward(row_block, w_one, w_two, w_proj)[1:]
        new_grads = tower_backward(upstream, w_one, w_two, w_proj, hidden, saved)
        return tuple(old_sum + new_part for old_sum, new_part in zip(running, new_grads)), None

    zeros_init = (jnp.zeros(w_one.shape, jnp.float32), jnp.zeros(w_two.shape, jnp.float32), jnp.zeros(w_proj.shape, jnp.float32))
    return lax.scan(body, zeros_init, (row_subs, up_subs))[0]


def local_step(q_loc, d_loc, value_a11, q_w1, q_w2, q_proj, d_w1, d_w2, d_proj):
    rows_loc, width_in = q_loc.shape
    q_sub = q_loc.reshape(SUB_COUNT, rows_loc // SUB_COUNT, width_in)
    d_sub = d_loc.reshape(SUB_COUNT, 2 * rows_loc // SUB_COUNT, width_in)
    q_reps = lax.map(lambda row_block: tower_forward(row_block, q_w1, q_w2, q_proj)[0], q_sub).reshape(rows_loc, -1)
    d_reps = lax.map(lambda row_block: tower_forward(row_block, d_w1, d_w2, d_proj)[0], d_sub).reshape(2, rows_loc, -1)
    all_docs = lax.all_gather(d_reps, 'data', axis=1, tiled=True)
    global_batch = all_docs.shape[1]
    rep_width = all_docs.shape[2]
    doc_flat = all_docs.reshape(2 * global_batch, rep_width)
    logits = lax.dot_general(q_reps, doc_flat, LAST_CONTRACT, preferred_element_type=jnp.float32) / value_a11
    row_start = lax.axis_index('data') * rows_loc
    target = jnp.arange(2 * global_batch)[None, :] == (row_start + jnp.arange(rows_loc))[:, None]
    log_norm = jax.nn.logsumexp(logits, axis=1)
    pos_logit = jnp.sum(jnp.where(target, logits, 0.0), axis=1)
    loss = lax.psum(jnp.sum(log_norm - pos_logit), 'data') / global_batch
    soft_prob = jnp.exp(logits - log_norm[:, None])
    grad_logit = ((soft_prob - target.astype(jnp.float32)) / (global_batch * value_a11)).astype(jnp.bfloat16)
    q_up = jnp.dot(grad_logit, doc_flat, preferred_element_type=jnp.float32).astype(jnp.bfloat16)
    doc_part = lax.dot_general(grad_logit, q_reps, ROWS_CONTRACT, preferred_element_type=jnp.float32)
    doc_up = lax.psum_scatter(doc_part.reshape(2, global_batch, rep_width), 'data', scatter_dimension=1, tiled=True).astype(jnp.bfloat16)
    q_grads = tower_grads(q_sub, q_up.reshape(SUB_COUNT, -1, rep_width), q_w1, q_w2, q_proj)
    d_grads = tower_grads(d_sub, doc_up.reshape(SUB_COUNT, -1, rep_width), d_w1, d_w2, d_proj)
    q_one, q_two, q_pgrad = lax.psum(q_grads, 'data')
    d_one, d_two, d_pgrad = lax.psum(d_grads, 'data')
    return (loss, q_one, q_two, q_pgrad, d_one, d_two, d_pgrad)


def solution(mesh):
    specs_in = (P('data', None), P(None, 'data', None), P(), P(), P(), P(), P(), P(), P())
    specs_out = (P(), P(), P(), P(), P(), P(), P())
    return jax.shard_map(local_step, mesh=mesh, in_specs=specs_in, out_specs=specs_out, check_vma=False)
```

profile of v0, /device:TPU:1, one launch (start us, length us, event | category | flops | bytes accessed | tf_op | source)
XLA Modules:
  0.0 1326.2 jit_solution(14240393232981905994)
XLA Ops:
  7.2 32.4 %while.57 = (s32[]{:T(128)}, bf16[4,32,512]{2,1,0:T(8,128)(2,1)}, bf16[4,32,512]{2,1,0:T(8,128)(2,1)}, bf16[2,512,2048]{2,1,0:T(8,128)(2,1)}, bf16[2,2048,512]{2...) while((s32[]{:T(128)}, bf16[4,32,512]{2,1,0:T(8,128)(2,1)}, bf16[4,32,512]{2,1,0:T(8,128)(2,1)}, ...), condition=%wide.region_3.4_spmd, body=%wide.region_2.3_spmd.sunk | while | flops 286507008 | bytes 11470441 | solution.py:57
  7.3 3.2 fusion.454
  12.5 2.8 fusion.456
  15.4 3.1 fusion.454
  20.6 2.8 fusion.456
  23.5 3.1 fusion.454
  28.7 2.8 fusion.456
  31.6 3.1 fusion.454
  36.8 2.8 fusion.456
  40.4 28.2 %while.56 = (s32[]{:T(128)}, bf16[4,16,512]{2,1,0:T(8,128)(2,1)S(1)}, bf16[4,16,512]{2,1,0:T(8,128)(2,1)}, bf16[2,512,2048]{2,1,0:T(8,128)(2,1)}, bf16[2,2048,51...) while((s32[]{:T(128)}, bf16[4,16,512]{2,1,0:T(8,128)(2,1)S(1)}, ...), condition=%wide.region_1.2_spmd, body=%wide.region_0.1_spmd.sunk | while | flops 143253504 | bytes 9143885 | solution.py:56
  40.4 2.9 fusion.443
  47.4 2.9 fusion.443
  54.5 2.9 fusion.443
  61.5 2.9 fusion.443
  68.6 55.2 %all-gather.2.cloned.1.call-done = bf16[2,8192,512]{2,1,0:T(8,128)(2,1)} async-done(((bf16[2,64,512]{2,1,0:T(8,128)(2,1)}), bf16[2,8192,512]{2,1,0:T(8,128)(2,1)}) %all-gather.2.cloned.1.call-update) | async-done | bytes 16777232 | tf_op jit(solution)/shard_map/all_gather | solution.py:58
  123.7 13.1 fusion.336
  136.8 3.5 select_reduce_fusion
  142.0 13.1 fusion.329
  155.5 10.1 fusion.335
  165.6 150.8 %while.58 = (s32[]{:T(128)}, f32[2,512,2048]{2,1,0:T(8,128)}, f32[2,2048,512]{2,1,0:T(8,128)}, f32[512,512]{1,0:T(8,128)S(1)}, bf16[4,16,512]{2,1,0:T(8,128)(2,1...) while((s32[]{:T(128)}, f32[2,512,2048]{2,1,0:T(8,128)}, ...), condition=%wide.region_10.11_spmd.clone, body=%wide.region_9.10_spmd.clone.sunk | while | flops 401555456 | bytes 136841488 | solution.py:49
  173.5 2.7 convolution_bitcast_fusion.19
  176.3 2.8 convolution_bitcast_fusion.18
  179.1 6.7 maximum_add_fusion.9
  185.8 4.9 convolution_bitcast_fusion.17
  192.9 4.2 maximum_add_fusion.8
  207.4 2.7 convolution_bitcast_fusion.19
  210.2 2.8 convolution_bitcast_fusion.18
  213.0 9.6 maximum_add_fusion.9
  222.5 4.9 convolution_bitcast_fusion.17
  229.7 6.5 maximum_add_fusion.8
  246.4 2.7 convolution_bitcast_fusion.19
  249.1 2.8 convolution_bitcast_fusion.18
  251.9 9.6 maximum_add_fusion.9
  261.5 4.9 convolution_bitcast_fusion.17
  268.6 6.5 maximum_add_fusion.8
  285.3 2.7 convolution_bitcast_fusion.19
  288.1 2.8 convolution_bitcast_fusion.18
  290.9 9.6 maximum_add_fusion.9
  300.5 4.9 convolution_bitcast_fusion.17
  307.6 6.5 maximum_add_fusion.8
  316.4 529.6 %reduce-scatter.2.cloned.1.call-done = f32[2,64,512]{2,1,0:T(8,128)} async-done(((f32[2,8192,512]{2,1,0:T(8,128)}), f32[2,64,512]{2,1,0:T(8,128)}) %reduce-scatter.2.cloned.1.call-update) | async-done | bytes 262160 | tf_op jit(solution)/shard_map/reduce_scatter | solution.py:72
  847.0 151.9 %while.59 = (s32[]{:T(128)}, f32[2,512,2048]{2,1,0:T(8,128)}, f32[2,2048,512]{2,1,0:T(8,128)}, f32[512,512]{1,0:T(8,128)S(1)}, bf16[4,32,512]{2,1,0:T(8,128)(2,1...) while((s32[]{:T(128)}, f32[2,512,2048]{2,1,0:T(8,128)}, ...), condition=%wide.region_16.17_spmd.clone, body=%wide.region_15.16_spmd.clone.sunk | while | flops 790003712 | bytes 137890000 | solution.py:49
  855.5 2.8 convolution_bitcast_fusion.23
  861.0 6.7 maximum_add_fusion.11
  867.7 4.8 convolution_bitcast_fusion.21
  874.7 4.2 maximum_add_fusion.10
  889.7 2.8 convolution_bitcast_fusion.23
  895.1 9.6 maximum_add_fusion.11
  904.7 4.8 convolution_bitcast_fusion.21
  911.7 6.4 maximum_add_fusion.10
  928.8 2.8 convolution_bitcast_fusion.23
  934.3 9.6 maximum_add_fusion.11
  943.9 4.8 convolution_bitcast_fusion.21
  950.9 6.4 maximum_add_fusion.10
  968.0 2.8 convolution_bitcast_fusion.23
  973.5 9.6 maximum_add_fusion.11
  983.0 4.8 convolution_bitcast_fusion.21
  990.1 6.4 maximum_add_fusion.10
  999.9 70.8 %psum.49 = f32[]{:T(128)} all-reduce(f32[]{:T(128)} %get-tuple-element.485), channel_id=1, replica_groups=mesh['data'=128] {'data'}, use_global_device_ids=true, to_apply=%region_8.9 | all-reduce | flops 1 | bytes 8 | tf_op jit(solution)/shard_map/psum | solution.py:67
  1071.3 222.4 %all-reduce.3.cloned.1.call-done = (f32[2,512,2048]{2,1,0:T(8,128)}, f32[2,2048,512]{2,1,0:T(8,128)}, f32[512,512]{1,0:T(8,128)}, f32[2,512,2048]{2,1,0:T(8,128)...) async-done(((f32[2,512,2048]{2,1,0:T(8,128)}, f32[2,2048,512]{2,1,0:T(8,128)}, f32[512,512]{1,0:T(8,128)}, f32[2,512,2048]{2,1,0:T(8,128)}, f32[2,2048,512]{2,1,0:T(8,128)}, ...) | async-done | bytes 35651600 | tf_op jit(solution)/shard_map/psum | solution.py:75
  1293.7 8.9 copy.67
  1302.6 4.3 copy.68
  1308.8 4.2 copy.70
  1314.2 3.4 copy.71
  (199 shorter events, 144.7 us)
Async XLA Ops:
  7.2 116.6 %all-gather.2.cloned.1.call-start = ((), (), s32[]{:S(2)}) async-start(), calls=%async_computation.1 | async-start | bytes 16908288 | tf_op jit(solution)/shard_map/all_gather | solution.py:58
  7.2 33.2 %copy-start.6 = (bf16[512,512]{1,0:T(8,128)(2,1)S(1)}, bf16[512,512]{1,0:T(8,128)(2,1)}, u32[]{:S(2)}) copy-start(bf16[512,512]{1,0:T(8,128)(2,1)} %param.22) | copy-start | bytes 1572868
  7.2 5.3 copy-start.7
  15.4 5.2 copy-start.7
  23.5 5.2 copy-start.7
  31.6 5.2 copy-start.7
  39.7 806.4 %reduce-scatter.2.cloned.1.call-start = ((), (), s32[]{:S(2)}) async-start(), calls=%async_computation.2 | async-start | bytes 33816576 | tf_op jit(solution)/shard_map/reduce_scatter | solution.py:72
  136.8 4.1 copy-start.11
  155.2 1138.5 %all-reduce.3.cloned.1.call-start = ((), (), s32[]{:S(2)}) async-start(), calls=%async_computation.3 | async-start | bytes 71303168 | tf_op jit(solution)/shard_map/psum | solution.py:75
  165.6 681.4 %copy-start.8 = (bf16[512,512]{1,0:T(8,128)(2,1)S(1)}, bf16[512,512]{1,0:T(8,128)(2,1)}, u32[]{:S(2)}) copy-start(bf16[512,512]{1,0:T(8,128)(2,1)} %get-tuple-element.814) | copy-start | bytes 1572868
  165.7 6.3 copy-start.15
  165.7 6.5 copy-start.2
  167.8 5.1 copy-start.3
  190.7 2.2 copy-start
  192.9 4.2 copy-start.16
  199.5 6.3 copy-start.15
  199.5 6.5 copy-start.2
  201.7 5.1 copy-start.3
  227.5 2.2 copy-start
  229.6 6.5 copy-start.16
  238.5 6.3 copy-start.15
  238.5 6.5 copy-start.2
  240.7 5.1 copy-start.3
  266.4 2.2 copy-start
  268.6 6.5 copy-start.16
  277.5 6.3 copy-start.15
  277.5 6.5 copy-start.2
  279.6 5.1 copy-start.3
  305.4 2.2 copy-start
  307.6 6.5 copy-start.16
  316.4 530.6 %copy-start.10 = (f32[512,512]{1,0:T(8,128)}, f32[512,512]{1,0:T(8,128)S(1)}, u32[]{:S(2)}) copy-start(f32[512,512]{1,0:T(8,128)S(1)} %get-tuple-element.353) | copy-start | bytes 3145732
  847.3 6.7 copy-start.4
  849.5 5.3 copy-start.5
  872.5 2.2 copy-start.1
  881.4 6.7 copy-start.4
  883.6 5.3 copy-start.5
  909.5 2.2 copy-start.1
  920.6 6.7 copy-start.4
  922.8 5.3 copy-start.5
  948.7 2.2 copy-start.1
  959.7 6.7 copy-start.4
  962.0 5.3 copy-start.5
  987.9 2.2 copy-start.1
  998.9 1.0 copy-start.9
  1293.7 8.9 copy-start.12
  1293.7 14.1 %slice-start.2 = ((s8[8388608]{0:T(1024)(128)(4,1)}), s8[4194304]{0:T(1024)(128)(4,1)S(1)}, s32[]{:S(2)}) async-start(s8[8388608]{0:T(1024)(128)(4,1)} %bitcast.372), calls=%async_computation.6 | async-start | bytes 8388608
  1302.6 4.3 copy-start.14
  1302.6 6.2 slice-start.3
  1306.8 6.2 slice-start
  1308.8 5.4 slice-start.1
  1314.2 3.4 copy-start.13
Sparse Core Ops, SparseCore 0:
  39.8 83.8 all-gather.1
  155.3 690.6 reduce-scatter.1
  1000.0 293.6 all-reduce.2
where the time goes:
time: 1330 us
  waiting for transfers between devices  807 us (61%)
  matrix products  269 us (20%)
  other arithmetic  124 us (9%)
  blocking collectives  70.8 us (5%)
  local copies, waits for them, and re-layouts  37.7 us (3%)
  between operations  16.4 us (1%)
    reduce_scatter x1, waiting for transfers between devices, local_step(): lax.psum_scatter(doc_part.reshape(2, global_batch, rep_width), 'data', sc...  530 us
    psum x1, waiting for transfers between devices, local_step(): q_one, q_two, q_pgrad = lax.psum(q_grads, 'data')  222 us
    add x16, other arithmetic, body(): old_sum + new_part  118 us
    psum x1, blocking collectives, local_step(): loss = lax.psum(jnp.sum(log_norm - pos_logit), 'data') / global_batch  70.8 us
    all_gather x1, waiting for transfers between devices, local_step(): all_docs = lax.all_gather(d_reps, 'data', axis=1, tiled=True)  55.2 us
    dot_general x24, matrix products, tower_forward(): pre_act = jnp.dot(hidden, w_one[layer], preferred_element_type=jnp.float32)  50 us
    dot_general x16, matrix products, tower_backward(): lax.dot_general(h_in, pre_grad, ROWS_CONTRACT, preferred_element_type=jnp...  44.8 us
    dot_general x16, matrix products, tower_backward(): lax.dot_general(act_bf, resid_bf, ROWS_CONTRACT, preferred_element_type=j...  44.1 us
  transfers between devices with their start and end apart: 3, of which 3 were waited for; matrix products, arithmetic and copies ran while one was open for 14% of the time, Pallas kernels for 0%

commit v1 on v0

v1 whole, which is shorter than its diff:
```python
import functools

import jax
import jax.numpy as jnp
from jax import lax
from jax.experimental import pallas as pl
from jax.experimental.pallas import tpu as pltpu
from jax.sharding import PartitionSpec as P

F32 = jnp.float32
BF16 = jnp.bfloat16
MESH = pl.DeviceIdType.MESH
SUB_COUNT = 4
SIDE = 4
ROWS_CONTRACT = (((0,), (0,)), ((), ()))
LAST_CONTRACT = (((1,), (1,)), ((), ()))
VMEM_LIMIT = 67043328

UNITS = 1088
COLOUR_OFFSET = (0, 384, 768)
COLOUR_ROWS = (6, 6, 5)
COLOUR_DIMS = (('x', 'y', 'z'), ('y', 'z', 'x'), ('z', 'x', 'y'))


def place():
    me = lax.axis_index('data')
    core = lax.rem(me, 2)
    x = lax.rem(me // 2, SIDE)
    y = lax.rem(me // 8, SIDE)
    z = me // 32
    return dict(z=z, y=y, x=x, core=core)


def device(at):
    return (((at['z'] * SIDE + at['y']) * SIDE + at['x']) * 2 + at['core'],)


def moved(at, dim, step):
    size = 2 if dim == 'core' else SIDE
    return {**at, dim: lax.rem(at[dim] + step, size)}


def dot(lhs, rhs, dims=None):
    if dims is None:
        return jnp.dot(lhs, rhs, preferred_element_type=F32)
    return lax.dot_general(lhs, rhs, dims, preferred_element_type=F32)


def tower_forward(rows, w_one, w_two, w_proj):
    hidden = rows
    for layer in range(2):
        act = jax.nn.gelu(dot(hidden, w_one[layer])).astype(BF16)
        hidden = (hidden.astype(F32) + dot(act, w_two[layer])).astype(BF16)
    return dot(hidden, w_proj[...]).astype(BF16)


def forward_kernel(q_in, d_in, q_w1, q_w2, q_proj, d_w1, d_w2, d_proj, q_out, d_out):
    def body(sub, carry):
        rows = pl.ds(pl.multiple_of(sub * 16, 16), 16)
        q_out[rows, :] = tower_forward(q_in[rows, :], q_w1, q_w2, q_proj)
        rows = pl.ds(pl.multiple_of(sub * 32, 32), 32)
        d_out[rows, :] = tower_forward(d_in[rows, :], d_w1, d_w2, d_proj)
        return carry

    lax.fori_loop(0, SUB_COUNT, body, 0)


def forward(q_rows, d_rows, weights):
    vmem = pl.BlockSpec(memory_space=pltpu.VMEM)
    return pl.pallas_call(
        forward_kernel,
        out_shape=(jax.ShapeDtypeStruct(q_rows.shape, BF16), jax.ShapeDtypeStruct(d_rows.shape, BF16)),
        in_specs=[vmem] * 8,
        out_specs=(vmem, vmem),
        compiler_params=pltpu.CompilerParams(vmem_limit_bytes=VMEM_LIMIT),
        name='towers_forward',
    )(q_rows, d_rows, *weights)


def score_kernel(tau_ref, q_ref, d_ref, q_up, d_up, loss_ref, q_all, d_all, st, stats, q_part, d_part, q_sum, d_sum, loss_all, send, recv):
    at = place()
    q_slot = at['y'] * SIDE + at['x']
    d_slot = at['z'] * 2 + at['core']
    q_peers = [moved(moved(at, 'x', s % SIDE), 'y', s // SIDE) for s in range(1, 16)]
    d_peers = [moved(moved(at, 'core', s % 2), 'z', s // 2) for s in range(1, 8)]

    barrier = pltpu.get_barrier_semaphore()
    for peer in q_peers + d_peers:
        pl.semaphore_signal(barrier, inc=1, device_id=device(peer), device_id_type=MESH)

    q_all[q_slot] = q_ref[...]
    d_all[d_slot] = d_ref[...]
    pl.semaphore_wait(barrier, len(q_peers) + len(d_peers))

    count = [0]
    started = []

    def copy(src, dst, peer):
        k = count[0]
        count[0] += 1
        c = pltpu.make_async_remote_copy(src_ref=src, dst_ref=dst, send_sem=send.at[k], recv_sem=recv.at[k], device_id=device(peer), device_id_type=MESH)
        c.start()
        started.append(c)
        return c

    gathers = [copy(d_ref, d_all.at[d_slot], p) for p in d_peers]
    gathers += [copy(q_ref, q_all.at[q_slot], p) for p in q_peers]
    for c in gathers:
        c.wait_recv()

    tau = tau_ref[0]
    queries = q_all[...].reshape(1024, 512)
    highs, sums = [], []
    for b in range(8):
        tile = dot(d_all[b], queries, LAST_CONTRACT) / tau
        st[b] = tile
        highs.append(jnp.max(tile, axis=0, keepdims=True))
    high = functools.reduce(jnp.maximum, highs)
    total = jnp.zeros_like(high)
    for b in range(8):
        total = total + jnp.sum(jnp.exp(st[b] - high), axis=0, keepdims=True)
    column = lax.broadcasted_iota(jnp.int32, (64, 1024), 1)
    row = lax.broadcasted_iota(jnp.int32, (64, 1024), 0)
    target = column == row + q_slot * 64
    own = st[d_slot, 0:64, :]
    positive = jnp.sum(jnp.where(target, own, 0.0), axis=0, keepdims=True)
    stats[q_slot, 0:1, :] = high
    stats[q_slot, 1:2, :] = total
    stats[q_slot, 2:3, :] = positive
    shares = [copy(stats.at[q_slot], stats.at[q_slot], p) for p in q_peers]
    for c in shares:
        c.wait_recv()
    all_stats = [stats[j] for j in range(16)]
    top = functools.reduce(jnp.maximum, [s[0:1] for s in all_stats])
    norm = sum(s[1:2] * jnp.exp(s[0:1] - top) for s in all_stats)
    log_norm = top + jnp.log(norm)
    positives = sum(s[2:3] for s in all_stats)
    part = jnp.sum(log_norm - positives, axis=1, keepdims=True)
    loss_all[d_slot] = jnp.broadcast_to(part, (8, 128))
    losses = [copy(loss_all.at[d_slot], loss_all.at[d_slot], p) for p in d_peers]

    scale = 8192.0 * tau
    d_row = lax.broadcasted_iota(jnp.int32, (128, 1024), 0)
    d_col = lax.broadcasted_iota(jnp.int32, (128, 1024), 1)
    grads = []
    for b in range(8):
        hit = (d_col == d_row + q_slot * 64) & (d_row < 64) & (d_slot == b)
        grads.append(((jnp.exp(st[b] - log_norm) - jnp.where(hit, 1.0, 0.0)) / scale).astype(BF16))
    for b in range(8):
        d_part[b] = dot(grads[b], queries)
    d_moves = [copy(d_part.at[p['z'] * 2 + p['core']], d_sum.at[d_slot], p) for p in d_peers]
    grad = jnp.concatenate(grads, axis=0)
    docs = d_all[...].reshape(1024, 512)
    q_part[...] = dot(grad, docs, ROWS_CONTRACT).reshape(16, 64, 512)
    q_moves = [copy(q_part.at[p['y'] * SIDE + p['x']], q_sum.at[q_slot], p) for p in q_peers]
    d_sum[d_slot] = d_part[d_slot]
    q_sum[q_slot] = q_part[q_slot]
    for c in losses:
        c.wait_recv()
    loss_ref[...] = sum(loss_all[j] for j in range(8)) / 8192.0
    for c in d_moves:
        c.wait_recv()
    d_up[...] = sum(d_sum[j] for j in range(8)).astype(BF16)
    for c in q_moves:
        c.wait_recv()
    q_up[...] = sum(q_sum[j] for j in range(16)).astype(BF16)
    for c in started:
        c.wait_send()


def scores(tau, q_reps, d_reps):
    vmem = pl.BlockSpec(memory_space=pltpu.VMEM)
    copies = 3 * 15 + 3 * 7
    return pl.pallas_call(
        score_kernel,
        out_shape=(
            jax.ShapeDtypeStruct((64, 512), BF16),
            jax.ShapeDtypeStruct((128, 512), BF16),
            jax.ShapeDtypeStruct((8, 128), F32),
        ),
        in_specs=[pl.BlockSpec(memory_space=pltpu.SMEM), vmem, vmem],
        out_specs=(vmem, vmem, vmem),
        scratch_shapes=[
            pltpu.VMEM((16, 64, 512), BF16),
            pltpu.VMEM((8, 128, 512), BF16),
            pltpu.VMEM((8, 128, 1024), F32),
            pltpu.VMEM((16, 3, 1024), F32),
            pltpu.VMEM((16, 64, 512), F32),
            pltpu.VMEM((8, 128, 512), F32),
            pltpu.VMEM((16, 64, 512), F32),
            pltpu.VMEM((8, 128, 512), F32),
            pltpu.VMEM((8, 8, 128), F32),
            pltpu.SemaphoreType.DMA((copies,)),
            pltpu.SemaphoreType.DMA((copies,)),
        ],
        compiler_params=pltpu.CompilerParams(collective_id=0, has_side_effects=True, vmem_limit_bytes=VMEM_LIMIT),
        name='scores',
    )(tau, q_reps, d_reps)


def gelu_back(pre, act_grad):
    return jax.vjp(jax.nn.gelu, pre)[1](act_grad)[0]


def tower_backward(sub, rows_per, x_ref, up_ref, w_one, w_two, w_proj, acc, pre_s, act_s):
    rows = pl.ds(pl.multiple_of(sub * rows_per, rows_per), rows_per)
    hidden = [x_ref[rows, :]]
    for layer in range(2):
        pre = dot(hidden[layer], w_one[layer])
        pre_s[layer, 0:rows_per] = pre
        act = jax.nn.gelu(pre).astype(BF16)
        act_s[layer, 0:rows_per] = act
        hidden.append((hidden[layer].astype(F32) + dot(act, w_two[layer])).astype(BF16))
    up = up_ref[rows, :]

    def add(base, lhs, rhs):
        for i in range(lhs.shape[1] // 256):
            part = dot(lhs[:, i * 256:(i + 1) * 256], rhs, ROWS_CONTRACT).reshape(32, 8, 512)
            at = base + i * 32
            acc[at:at + 32] += part

    add(1024, hidden[2], up)
    resid = dot(up, w_proj[...], LAST_CONTRACT)
    for layer in (1, 0):
        resid_bf = resid.astype(BF16)
        add(512 + layer * 256, act_s[layer, 0:rows_per], resid_bf)
        act_grad = dot(resid_bf, w_two[layer], LAST_CONTRACT)
        pre_grad = gelu_back(pre_s[layer, 0:rows_per], act_grad).astype(BF16)
        for c in range(4):
            add(layer * 256 + c * 64, hidden[layer], pre_grad[:, c * 512:(c + 1) * 512])
        if layer == 1:
            resid = resid + dot(pre_grad, w_one[layer], LAST_CONTRACT)


def backward_kernel(q_in, d_in, q_up, d_up, q_w1, q_w2, q_proj, d_w1, d_w2, d_proj, out, q_acc, d_acc, pre_s, act_s, sems):
    def clear(i, carry):
        q_acc[pl.ds(i * 8, 8)] = jnp.zeros((8, 8, 512), F32)
        d_acc[pl.ds(i * 8, 8)] = jnp.zeros((8, 8, 512), F32)
        return carry

    lax.fori_loop(0, UNITS // 8, clear, 0)

    def q_body(sub, carry):
        tower_backward(sub, 16, q_in, q_up, q_w1, q_w2, q_proj, q_acc, pre_s, act_s)
        return carry

    lax.fori_loop(0, SUB_COUNT, q_body, 0)
    q_copy = pltpu.make_async_copy(q_acc, out.at[0], sems.at[0])
    q_copy.start()

    def d_body(sub, carry):
        tower_backward(sub, 32, d_in, d_up, d_w1, d_w2, d_proj, d_acc, pre_s, act_s)
        return carry

    lax.fori_loop(0, SUB_COUNT, d_body, 0)
    d_copy = pltpu.make_async_copy(d_acc, out.at[1], sems.at[1])
    d_copy.start()
    q_copy.wait()
    d_copy.wait()


def backward(q_rows, d_rows, q_up, d_up, weights):
    vmem = pl.BlockSpec(memory_space=pltpu.VMEM)
    return pl.pallas_call(
        backward_kernel,
        out_shape=jax.ShapeDtypeStruct((2, UNITS, 8, 512), F32),
        in_specs=[vmem] * 10,
        out_specs=pl.BlockSpec(memory_space=pl.ANY),
        scratch_shapes=[
            pltpu.VMEM((UNITS, 8, 512), F32),
            pltpu.VMEM((UNITS, 8, 512), F32),
            pltpu.VMEM((2, 32, 2048), F32),
            pltpu.VMEM((2, 32, 2048), BF16),
            pltpu.SemaphoreType.DMA((2,)),
        ],
        compiler_params=pltpu.CompilerParams(vmem_limit_bytes=VMEM_LIMIT),
        name='towers_backward',
    )(q_rows, d_rows, q_up, d_up, *weights)


def add_into(dst, dst_at, pieces, size):
    step = next(s for s in (8, 6, 5, 4, 3, 2, 1) if size % s == 0)

    def body(i, carry):
        here = pl.ds(dst_at + i * step, step)
        total = dst[here]
        for ref, ref_at in pieces:
            total = total + ref[pl.ds(ref_at + i * step, step)]
        dst[here] = total
        return carry

    lax.fori_loop(0, size // step, body, 0)


def reduce_kernel(grads, out, mine, pair, *rest):
    bufs, (load_sem, pair_send, pair_recv, rs_send, rs_recv, ag_send, ag_recv, core_send, core_recv) = rest[:12], rest[12:]
    at = place()
    core = at['core']
    other = moved(at, 'core', 1)
    barrier = pltpu.get_barrier_semaphore()
    peers = [other] + [moved(at, d, s) for d in 'xyz' for s in (1, 3)]
    for peer in peers:
        pl.semaphore_signal(barrier, inc=1, device_id=device(peer), device_id_type=MESH)
    pl.semaphore_wait(barrier, len(peers))
    unsent = []

    def remote(src, dst, send, recv, peer):
        c = pltpu.make_async_remote_copy(src_ref=src, dst_ref=dst, send_sem=send, recv_sem=recv, device_id=device(peer), device_id_type=MESH)
        c.start()
        unsent.append(c)
        return c

    loads, pairs = {}, {}
    for rel in (2, 1, 3, 0):
        for k in range(3):
            n = 16 * COLOUR_ROWS[k]
            spot = COLOUR_OFFSET[k] + lax.rem(at[COLOUR_DIMS[k][0]] + rel, SIDE) * n
            here = pl.ds(spot, n)
            pairs[k, rel] = remote(grads.at[1 - core, here], pair.at[here], pair_send.at[k * 4 + rel], pair_recv.at[k * 4 + rel], other)
            load = pltpu.make_async_copy(grads.at[core, here], mine.at[here], load_sem.at[k * 4 + rel])
            load.start()
            loads[k, rel] = load

    def settle(k, rel):
        n = 16 * COLOUR_ROWS[k]
        spot = COLOUR_OFFSET[k] + lax.rem(at[COLOUR_DIMS[k][0]] + rel, SIDE) * n
        loads[k, rel].wait()
        pairs[k, rel].wait_recv()
        add_into(mine, spot, [(pair, spot)], n)

    base = list(COLOUR_OFFSET)

    def ring(k, p):
        dim = COLOUR_DIMS[k][p]
        n = COLOUR_ROWS[k] * (16, 4, 1)[p]
        half = (n + 1) // 2
        spot = [base[k] + lax.rem(at[dim] + rel, SIDE) * n for rel in range(4)]
        return dim, n, half, spot, moved(at, dim, 1), moved(at, dim, 3)

    moves = {}

    def rs_copy(k, p, m, src, dst, peer):
        s = (k * 3 + p) * 6 + m
        moves[k, p, m] = remote(src, dst, rs_send.at[s], rs_recv.at[s], peer)

    def rs_far(k, p):
        dim, n, half, spot, right, left = ring(k, p)
        tr = bufs[p * 4]
        tl = bufs[p * 4 + 1]
        o, oh = COLOUR_OFFSET[k] // 64 * (16, 4, 1)[p], half_offset(k, p)
        rs_copy(k, p, 0, mine.at[pl.ds(spot[2], half)], tr.at[pl.ds(oh, half)], right)
        rs_copy(k, p, 1, mine.at[pl.ds(spot[2] + half, n - half)], tl.at[pl.ds(oh, n - half)], left)

    def rs_near(k, p):
        dim, n, half, spot, right, left = ring(k, p)
        fl, fr = bufs[p * 4 + 2], bufs[p * 4 + 3]
        o = COLOUR_OFFSET[k] // 64 * (16, 4, 1)[p]
        rs_copy(k, p, 2, mine.at[pl.ds(spot[1] + half, n - half)], fl.at[pl.ds(o + half, n - half)], right)
        rs_copy(k, p, 3, mine.at[pl.ds(spot[3], half)], fr.at[pl.ds(o, half)], left)

    def rs_pass(k, p):
        dim, n, half, spot, right, left = ring(k, p)
        tr, tl, fl, fr = bufs[p * 4:p * 4 + 4]
        o, oh = COLOUR_OFFSET[k] // 64 * (16, 4, 1)[p], half_offset(k, p)
        moves[k, p, 0].wait_recv()
        add_into(mine, spot[1], [(tr, oh)], half)
        rs_copy(k, p, 4, mine.at[pl.ds(spot[1], half)], fl.at[pl.ds(o, half)], right)
        moves[k, p, 1].wait_recv()
        add_into(mine, spot[3] + half, [(tl, oh)], n - half)
        rs_copy(k, p, 5, mine.at[pl.ds(spot[3] + half, n - half)], fr.at[pl.ds(o + half, n - half)], left)

    def rs_end(k, p):
        dim, n, half, spot, right, left = ring(k, p)
        fl, fr = bufs[p * 4 + 2], bufs[p * 4 + 3]
        o = COLOUR_OFFSET[k] // 64 * (16, 4, 1)[p]
        for m in (2, 3, 4, 5):
            moves[k, p, m].wait_recv()
        add_into(mine, spot[0], [(fl, o), (fr, o)], n)
        base[k] = spot[0]

    for k in range(3):
        settle(k, 2)
        rs_far(k, 0)
    for k in range(3):
        settle(k, 1)
        settle(k, 3)
        rs_near(k, 0)
    for k in range(3):
        rs_pass(k, 0)
    for k in range(3):
        settle(k, 0)
    bases = [[] for _ in range(3)]
    for p in range(3):
        for k in range(3):
            bases[k].append(base[k])
            rs_end(k, p)
            if p < 2:
                rs_far(k, p + 1)
                rs_near(k, p + 1)
        if p < 2:
            for k in range(3):
                rs_pass(k, p + 1)

    core_moves = []
    locals_ = []

    def hand(src, spot, n):
        i = len(core_moves)
        core_moves.append(remote(src, out.at[core, pl.ds(spot, n)], core_send.at[i], core_recv.at[i], other))

    gathers = {}

    def ag_copy(k, p, m, src, spot, n, peer):
        s = (k * 3 + p) * 6 + m
        gathers[k, p, m] = remote(src, out.at[core, pl.ds(spot, n)], ag_send.at[s], ag_recv.at[s], peer)

    def ag_start(k, p):
        base[k] = bases[k][p]
        dim, n, half, spot, right, left = ring(k, p)
        src = mine if p == 2 else out.at[core]
        first = src.at[pl.ds(spot[0], half)]
        second = src.at[pl.ds(spot[0] + half, n - half)]
        ag_copy(k, p, 0, first, spot[0], half, right)
        ag_copy(k, p, 1, second, spot[0] + half, n - half, left)
        ag_copy(k, p, 2, second, spot[0] + half, n - half, right)
        ag_copy(k, p, 3, first, spot[0], half, left)

    def ag_pass(k, p):
        base[k] = bases[k][p]
        dim, n, half, spot, right, left = ring(k, p)
        gathers[k, p, 0].wait_recv()
        ag_copy(k, p, 4, out.at[core, pl.ds(spot[3], half)], spot[3], half, right)
        gathers[k, p, 1].wait_recv()
        ag_copy(k, p, 5, out.at[core, pl.ds(spot[1] + half, n - half)], spot[1] + half, n - half, left)
        gathers[k, p, 2].wait_recv()
        hand(out.at[core, pl.ds(spot[3], n)], spot[3], n)
        gathers[k, p, 3].wait_recv()
        hand(out.at[core, pl.ds(spot[1], n)], spot[1], n)

    def ag_end(k, p):
        base[k] = bases[k][p]
        dim, n, half, spot, right, left = ring(k, p)
        gathers[k, p, 4].wait_recv()
        hand(out.at[core, pl.ds(spot[2], half)], spot[2], half)
        gathers[k, p, 5].wait_recv()
        hand(out.at[core, pl.ds(spot[2] + half, n - half)], spot[2] + half, n - half)

    for k in range(3):
        n, spot = COLOUR_ROWS[k], base[k]
        ag_start(k, 2)
        hand(mine.at[pl.ds(spot, n)], spot, n)
        local = pltpu.make_async_copy(mine.at[pl.ds(spot, n)], out.at[core, pl.ds(spot, n)], load_sem.at[12 + k])
        local.start()
        locals_.append(local)
    for p in (2, 1, 0):
        for k in range(3):
            ag_pass(k, p)
        for k in range(3):
            ag_end(k, p)
            if p == 2:
                locals_[k].wait()
            if p > 0:
                ag_start(k, p - 1)
    for c in core_moves:
        c.wait_recv()
    for c in unsent:
        c.wait_send()


def half_offset(k, p):
    sizes = [(r * (16, 4, 1)[p] + 1) // 2 for r in COLOUR_ROWS]
    return sum(sizes[:k])


def all_reduce(grads):
    scale = (16, 4, 1)
    bufs = []
    for p in range(3):
        halves = sum((r * scale[p] + 1) // 2 for r in COLOUR_ROWS)
        full = sum(COLOUR_ROWS) * scale[p]
        bufs += [pltpu.VMEM((n, 8, 512), F32) for n in (halves, halves, full, full)]
    dma = pltpu.SemaphoreType.DMA
    return pl.pallas_call(
        reduce_kernel,
        out_shape=jax.ShapeDtypeStruct(grads.shape, F32),
        in_specs=[pl.BlockSpec(memory_space=pl.ANY)],
        out_specs=pl.BlockSpec(memory_space=pl.ANY),
        scratch_shapes=[pltpu.VMEM((UNITS, 8, 512), F32), pltpu.VMEM((UNITS, 8, 512), F32)] + bufs
        + [dma((15,)), dma((12,)), dma((12,)), dma((54,)), dma((54,)), dma((54,)), dma((54,)), dma((39,)), dma((39,))],
        compiler_params=pltpu.CompilerParams(collective_id=1, has_side_effects=True, vmem_limit_bytes=VMEM_LIMIT),
        name='all_reduce',
    )(grads)


def unpack(total):
    w_one = total[:512].reshape(2, 4, 512, 512).transpose(0, 2, 1, 3).reshape(2, 512, 2048)
    w_two = total[512:1024].reshape(2, 2048, 512)
    return w_one, w_two, total[1024:].reshape(512, 512)


def local_step(q_loc, d_loc, temperature, *weights):
    d_rows = d_loc.reshape(-1, d_loc.shape[-1])
    q_reps, d_reps = forward(q_loc, d_rows, weights)
    q_up, d_up, loss = scores(temperature.reshape(1), q_reps, d_reps)
    total = all_reduce(backward(q_loc, d_rows, q_up, d_up, weights))
    return (loss[0, 0], *unpack(total[0]), *unpack(total[1]))


def solution(mesh):
    specs_in = (P('data', None), P(None, 'data', None), P(), P(), P(), P(), P(), P(), P())
    specs_out = (P(), P(), P(), P(), P(), P(), P())
    return jax.shard_map(local_step, mesh=mesh, in_specs=specs_in, out_specs=specs_out, check_vma=False)
```

time: 1330 us -> 360 us (0.27)
  waiting for transfers between devices: 807 us -> 0 us
  Pallas kernels: 0 us -> 320 us
  matrix products: 269 us -> 0 us
  other arithmetic: 124 us -> 0 us
  blocking collectives: 70.8 us -> 0 us
  between operations: 16.4 us -> 1.31 us
    reduce_scatter x1 -> x0, waiting for transfers between devices: 530 us -> none  [local_step(): lax.psum_scatter(doc_part.reshape(2, global_batch, rep_width), 'data', sc...]
    pallas_call x0 -> x4, Pallas kernels: none -> 320 us  [the longest x1 171 us: all_reduce(): pl.pallas_call(reduce_kernel, out_shape=jax.ShapeDtypeStruct(grads.shape,...]
    dot_general x115 -> x0, matrix products: 269 us -> none  [the longest x24 50 us: tower_forward(): pre_act = jnp.dot(hidden, w_one[layer], preferred_element_type=jnp.float32)]
    psum x1 -> x0, waiting for transfers between devices: 222 us -> none  [local_step(): q_one, q_two, q_pgrad = lax.psum(q_grads, 'data')]
    add x17 -> x0, other arithmetic: 118 us -> none  [the longest x16 118 us: body(): old_sum + new_part]
    psum x1 -> x0, blocking collectives: 70.8 us -> none  [local_step(): loss = lax.psum(jnp.sum(log_norm - pos_logit), 'data') / global_batch]
    all_gather x1 -> x0, waiting for transfers between devices: 55.2 us -> none  [local_step(): all_docs = lax.all_gather(d_reps, 'data', axis=1, tiled=True)]
    unnamed x30 -> x0, local copies, waits for them, and re-layouts: 25.9 us -> none
  transfers between devices with their start and end apart: 3 -> 0, of which waited for: 3 -> 0; matrix products, arithmetic and copies ran while one was open for 14% -> 0% of each run, Pallas kernels for 0% -> 0%
where the time goes in v1:
time: 360 us
  Pallas kernels  320 us (89%)
  local copies, waits for them, and re-layouts  38.4 us (11%)
    pallas_call x1, Pallas kernels, all_reduce(): pl.pallas_call(reduce_kernel, out_shape=jax.ShapeDtypeStruct(grads.shape,...  171 us
    pallas_call x1, Pallas kernels, scores(): pl.pallas_call(score_kernel, out_shape=(jax.ShapeDtypeStruct((64, 512), B...  67.8 us
    pallas_call x1, Pallas kernels, backward(): pl.pallas_call(backward_kernel, out_shape=jax.ShapeDtypeStruct((2, UNITS,...  62.2 us
    slice x1, local copies, waits for them, and re-layouts, unpack(): w_two = total[512:1024].reshape(2, 2048, 512)  21.5 us
    pallas_call x1, Pallas kernels, forward(): pl.pallas_call(forward_kernel, out_shape=(jax.ShapeDtypeStruct(q_rows.sha...  19.3 us
    reshape x2, local copies, waits for them, and re-layouts, unpack(): total[:512].reshape(2, 4, 512, 512).transpose(0, 2, 1, 3)  12.6 us

profile of v1, /device:TPU:1, one launch (start us, length us, event | category | flops | bytes accessed | tf_op | source)
XLA Modules:
  0.0 359.8 jit_solution(15191180344340625085)
XLA Ops:
  1.3 19.3 %towers_forward.1 = (bf16[64,512]{1,0:T(8,128)(2,1)}, bf16[128,512]{1,0:T(8,128)(2,1)}) custom-call(bf16[64,512]{1,0:T(8,128)(2,1)} %q_in.3, bf16[128,512]{1,0:T(8,128)(2,1)} %bitcast.26, bf16[2,512,2048]{2,1,0:T(8,128)(2,1)} %q_w1.3, bf16[2,2048,512]{2,1,0:T(8,128)(2,1)} %q_w2.3, bf16[512,512]{1,0:T(8,128)(2,1)} %q_proj.3, bf16[2,512,2048]{2,1,0:T(8,128)(2,1)} %d_w1.3, ...), custom_call_target="tpu_custom_call" | custom-call | tf_op jit(solution)/shard_map/towers_forward/pallas_call | solution.py:70
  20.6 67.8 %scores.1 = (bf16[64,512]{1,0:T(8,128)(2,1)}, bf16[128,512]{1,0:T(8,128)(2,1)}, f32[8,128]{1,0:T(8,128)}) custom-call(f32[1]{0:T(128)} %bitcast.19.tau_ref, bf16[64,512]{1,0:T(8,128)(2,1)} %get-tuple-element.12.q_ref, bf16[128,512]{1,0:T(8,128)(2,1)} %get-tuple-element.13.d_ref), custom_call_target="tpu_custom_call" | custom-call | tf_op jit(solution)/shard_map/scores/pallas_call | solution.py:174
  88.4 1.2 slice.35
  89.6 62.2 %towers_backward.1.grads = f32[2,1088,8,512]{3,2,1,0:T(8,128)} custom-call(bf16[64,512]{1,0:T(8,128)(2,1)} %q_in.3, bf16[128,512]{1,0:T(8,128)(2,1)} %bitcast.27, bf16[64,512]{1,0:T(8,128)(2,1)} %get-tuple-element.15.q_up, bf16[128,512]{1,0:T(8,128)(2,1)} %get-tuple-element.16.d_up, bf16[2,512,2048]{2,1,0:T(8,128)(2,1)} %q_w1.3, bf16[2,2048,512]{2,1,0:T(8,128)(2,1)} %q_w2.3, ...), custom_call_target="tpu_custom_call" | custom-call | tf_op jit(solution)/shard_map/towers_backward/pallas_call | solution.py:264
  151.8 170.7 %all_reduce.1 = f32[2,1088,8,512]{3,2,1,0:T(8,128)} custom-call(f32[2,1088,8,512]{3,2,1,0:T(8,128)} %towers_backward.1.grads), custom_call_target="tpu_custom_call" | custom-call | tf_op jit(solution)/shard_map/all_reduce/pallas_call | solution.py:483
  322.6 3.0 slice_bitcast_fusion
  325.6 21.5 %fusion = (f32[1,512,8,512]{3,2,1,0:T(8,128)}, f32[1,512,8,512]{3,2,1,0:T(8,128)}, f32[1,512,8,512]{3,2,1,0:T(8,128)}, f32[1,512,8,512]{3,2,1,0:T(8,128)S(1)}) fusion(f32[2,1088,8,512]{3,2,1,0:T(8,128)} %all_reduce.1), kind=kLoop, calls=%fused_computation.2 | loop fusion | bytes 67108864 | tf_op jit(solution)/shard_map/slice | solution.py:497
  347.1 8.2 %copy.19 = f32[2,4,64,8,512]{4,3,1,2,0:T(8,128)} copy(f32[2,4,64,8,512]{4,3,2,1,0:T(8,128)} %bitcast.21) | data formatting | bytes 16777216 | tf_op jit(solution)/shard_map/reshape | solution.py:496
  355.4 4.4 %copy.18 = f32[2,4,64,8,512]{4,3,1,2,0:T(8,128)} copy(f32[2,4,64,8,512]{4,3,2,1,0:T(8,128)S(1)} %bitcast.20) | data formatting | bytes 16777216 | tf_op jit(solution)/shard_map/reshape | solution.py:496

commit v2 on v0

v2 whole, which is shorter than its diff:
```python
import functools

import jax
import jax.numpy as jnp
from jax import lax
from jax.experimental import pallas as pl
from jax.experimental.pallas import tpu as pltpu
from jax.sharding import PartitionSpec as P

F32 = jnp.float32
BF16 = jnp.bfloat16
MESH = pl.DeviceIdType.MESH
SUB_COUNT = 4
SIDE = 4
ROWS_CONTRACT = (((0,), (0,)), ((), ()))
LAST_CONTRACT = (((1,), (1,)), ((), ()))
VMEM_LIMIT = 67043328

UNITS = 2176
HALF = 1088
TRAIN_VMEM = 27500000
PAIR_SLOT = (1, 1, 0, 0)
RING_SIZE = (16, 4, 1)
Q, D = range(2)
OUTER, MIDDLE, INNER = range(3)
OWN, RIGHT, ACROSS, LEFT = range(4)
MESSAGES = (
    (ACROSS, False, 0, 0), (ACROSS, True, 1, 0), (RIGHT, True, 0, 1), (LEFT, False, 1, 2), (RIGHT, False, 0, 1), (LEFT, True, 1, 2),
    (OWN, False, 0, None), (OWN, True, 1, None), (OWN, True, 0, None), (OWN, False, 1, None), (LEFT, False, 0, None), (RIGHT, True, 1, None),
)
ALL = tuple(range(len(MESSAGES)))
FAR, NEAR, ON, GATHER = ALL[:2], ALL[2:4], ALL[4:6], ALL[6:]
FIRST, SECOND, ONWARD = GATHER[:2], GATHER[2:4], GATHER[4:]
COLOURS = ((0, 6, ('x', 'y', 'z')), (384, 6, ('y', 'z', 'x')), (768, 5, ('z', 'x', 'y')))
HANDS = ((LEFT, False), (RIGHT, False), (ACROSS, False), (ACROSS, True), (OWN, False))


def place():
    me = lax.axis_index('data')
    core = lax.rem(me, 2)
    x = lax.rem(me // 2, SIDE)
    y = lax.rem(me // 8, SIDE)
    z = me // 32
    return dict(z=z, y=y, x=x, core=core)


def device(at):
    return (((at['z'] * SIDE + at['y']) * SIDE + at['x']) * 2 + at['core'],)


def moved(at, dim, step):
    size = 2 if dim == 'core' else SIDE
    return {**at, dim: lax.rem(at[dim] + step, size)}


def remote(src, dst, sems, index, peer):
    return pltpu.make_async_remote_copy(
        src_ref=src, dst_ref=dst, send_sem=sems[0].at[index], recv_sem=sems[1].at[index], device_id=device(peer), device_id_type=MESH
    )


def greet(peers):
    for peer in peers:
        pl.semaphore_signal(pltpu.get_barrier_semaphore(), inc=1, device_id=device(peer), device_id_type=MESH)


def dot(lhs, rhs, dims=None):
    if dims is None:
        return jnp.dot(lhs, rhs, preferred_element_type=F32)
    return lax.dot_general(lhs, rhs, dims, preferred_element_type=F32)


def add_into(dst, dst_at, pieces, size):
    step = next(s for s in (16, 12, 10, 8, 6, 5, 4, 3, 2, 1) if size % s == 0)

    def body(i, carry):
        here = pl.ds(dst_at + i * step, step)
        total = dst[here]
        for ref, ref_at in pieces:
            total = total + ref[pl.ds(ref_at + i * step, step)]
        dst[here] = total
        return carry

    lax.fori_loop(0, size // step, body, 0)


class Ring:
    def __init__(self, at, dim, x, base, n, buf, buf_at, sems, sem_at):
        self.x, self.n, self.buf, self.buf_at = x, n, buf, buf_at
        self.half = (n + 1) // 2
        self.rest = n - self.half
        self.spot = [base + lax.rem(at[dim] + rel, SIDE) * n for rel in range(SIDE)]
        self.peers = moved(at, dim, RIGHT), moved(at, dim, LEFT)
        self.sems, self.sem_at = sems, sem_at * len(MESSAGES)

    def copy(self, m):
        rel, second, way, slot = MESSAGES[m]
        shift, size = (self.half, self.rest) if second else (0, self.half)
        src = self.x.at[pl.ds(self.spot[rel] + shift, size)]
        dst = src if slot is None else self.buf.at[pl.ds(self.buf_at + slot * self.n + shift, size)]
        return remote(src, dst, self.sems, self.sem_at + m, self.peers[way])

    def start(self, which):
        for m in which:
            self.copy(m).start()

    def take(self, which):
        for m in which:
            self.copy(m).wait_recv()

    def sent(self, which):
        for m in which:
            self.copy(m).wait_send()

    def rs_pass(self):
        self.take(FAR[:1])
        add_into(self.x, self.spot[RIGHT], [(self.buf, self.buf_at)], self.half)
        self.start(ON[:1])
        self.take(FAR[1:])
        add_into(self.x, self.spot[LEFT] + self.half, [(self.buf, self.buf_at + self.half)], self.rest)
        self.start(ON[1:])

    def rs_end(self):
        self.take(NEAR + ON)
        got = [(self.buf, self.buf_at + slot * self.n) for slot in (1, 2)]
        add_into(self.x, self.spot[OWN], got, self.n)

    def ag_pass(self):
        for first, then in zip(GATHER[:2], GATHER[4:]):
            self.copy(first).wait_recv()
            self.copy(then).start()


def tower_forward(rows, w_one, w_two, w_proj):
    hidden = rows
    for layer in range(2):
        act = jax.nn.gelu(dot(hidden, w_one[layer])).astype(BF16)
        hidden = (hidden.astype(F32) + dot(act, w_two[layer])).astype(BF16)
    return dot(hidden, w_proj[...]).astype(BF16)


def forward_kernel(q_in, d_in, q_w1, q_w2, q_proj, d_w1, d_w2, d_proj, q_out, d_out):
    def body(sub, carry):
        rows = pl.ds(pl.multiple_of(sub * 16, 16), 16)
        q_out[rows, :] = tower_forward(q_in[rows, :], q_w1, q_w2, q_proj)
        rows = pl.ds(pl.multiple_of(sub * 32, 32), 32)
        d_out[rows, :] = tower_forward(d_in[rows, :], d_w1, d_w2, d_proj)
        return carry

    lax.fori_loop(0, SUB_COUNT, body, 0)


def forward(q_rows, d_rows, weights):
    vmem = pl.BlockSpec(memory_space=pltpu.VMEM)
    return pl.pallas_call(
        forward_kernel,
        out_shape=(jax.ShapeDtypeStruct(q_rows.shape, BF16), jax.ShapeDtypeStruct(d_rows.shape, BF16)),
        in_specs=[vmem] * 8,
        out_specs=(vmem, vmem),
        compiler_params=pltpu.CompilerParams(vmem_limit_bytes=VMEM_LIMIT),
        name='towers_forward',
    )(q_rows, d_rows, *weights)


def score_kernel(tau_ref, q_ref, d_ref, q_up, d_up, loss_ref, q_all, d_all, st, stats, q_part, d_part, q_buf, d_buf, pair, loss_all, *sems):
    at = place()
    core, z = at['core'], at['z']
    other = moved(at, 'core', 1)
    q_peers = [moved(moved(at, 'x', s % SIDE), 'y', s // SIDE) for s in range(1, 16)]
    d_peers = [moved(moved(at, 'core', s % 2), 'z', s // 2) for s in range(1, 8)]
    q_slot, d_slot = at['y'] * SIDE + at['x'], core * SIDE + z
    greet(q_peers + d_peers)

    outer, inner = ('y', 'x'), ('x', 'y')
    own = [at[outer[h]] * 8 + at[inner[h]] * 2 for h in range(2)]
    for h in range(2):
        q_all[h, pl.ds(own[h], 2)] = q_ref[h * 32:(h + 1) * 32, :].reshape(2, 16, 512)
    d_all[core, pl.ds(z * 8, 8)] = d_ref[...].reshape(8, 16, 512)

    def q_rings(x, h):
        wide = Ring(at, outer[h], x.at[h], 0, 8, q_buf.at[h], 0, sems, h)
        return wide, Ring(at, inner[h], x.at[h], at[outer[h]] * 8, 2, q_buf.at[h], 24, sems, 2 + h)

    q_wide, q_thin = zip(*[q_rings(q_all, h) for h in range(2)])
    docs_ring = Ring(at, 'z', d_all.at[core], 0, 8, d_buf, 0, sems, 4)
    hands_at = 5 * len(MESSAGES)
    pl.semaphore_wait(pltpu.get_barrier_semaphore(), len(q_peers) + len(d_peers))

    def hand(rel):
        here = d_all.at[core, pl.ds(docs_ring.spot[rel], 8)]
        return remote(here, here, sems, hands_at + rel, other)

    docs_ring.start(FIRST + SECOND)
    hand(OWN).start()
    for ring in q_thin:
        ring.start(FIRST + SECOND)
    for ring in q_thin:
        ring.ag_pass()
    docs_ring.ag_pass()
    for thin, wide in zip(q_thin, q_wide):
        thin.take(SECOND + ONWARD)
        wide.start(FIRST + SECOND)
    docs_ring.take(SECOND)
    hand(LEFT).start()
    hand(RIGHT).start()
    docs_ring.take(ONWARD)
    hand(ACROSS).start()
    for ring in q_wide:
        ring.ag_pass()
    for rel in range(SIDE):
        hand(rel).wait_recv()
    for ring in q_wide:
        ring.take(SECOND + ONWARD)

    tau = tau_ref[0]
    queries = q_all[...].reshape(1024, 512)
    blocks = [(c, j) for c in range(2) for j in range(SIDE)]

    def block(ref, c, j):
        return ref[c, j * 8:(j + 1) * 8].reshape(128, 512)

    highs = []
    for b, (c, j) in enumerate(blocks):
        tile = dot(block(d_all, c, j), queries, LAST_CONTRACT) / tau
        st[b] = tile
        highs.append(jnp.max(tile, axis=0, keepdims=True))
    high = functools.reduce(jnp.maximum, highs)
    total = sum(jnp.sum(jnp.exp(st[b] - high), axis=0, keepdims=True) for b in range(len(blocks)))

    def matches(rows):
        row = lax.broadcasted_iota(jnp.int32, (rows, 1024), 0)
        column = lax.broadcasted_iota(jnp.int32, (rows, 1024), 1)
        return (row < 64) & (column == jnp.where(row < 32, own[0] * 16 + row, 480 + own[1] * 16 + row))

    positive = jnp.sum(jnp.where(matches(64), st[d_slot, 0:64, :], 0.0), axis=0, keepdims=True)
    for i, row in enumerate((high, total, positive)):
        stats[q_slot, i:i + 1, :] = row
    extra = hands_at + SIDE
    shares = [remote(stats.at[q_slot], stats.at[q_slot], sems, extra + i, p) for i, p in enumerate(q_peers)]
    for c in shares:
        c.start()
    for c in shares:
        c.wait_recv()
    all_stats = [stats[j] for j in range(16)]
    top = functools.reduce(jnp.maximum, [s[0:1] for s in all_stats])
    norm = sum(s[1:2] * jnp.exp(s[0:1] - top) for s in all_stats)
    log_norm = top + jnp.log(norm)
    part = jnp.sum(log_norm - sum(s[2:3] for s in all_stats), axis=1, keepdims=True)
    loss_all[d_slot] = jnp.broadcast_to(part, (8, 128))
    extra = extra + len(shares)
    losses = [remote(loss_all.at[d_slot], loss_all.at[d_slot], sems, extra + i, p) for i, p in enumerate(d_peers)]
    for c in losses:
        c.start()

    scale = 8192.0 * tau
    hit = matches(128)
    grads = []
    for b in range(len(blocks)):
        soft = jnp.exp(st[b] - log_norm) - jnp.where(hit & (d_slot == b), 1.0, 0.0)
        grads.append((soft / scale).astype(BF16))
    grad = jnp.concatenate(grads, axis=0)
    docs = d_all[...].reshape(1024, 512)
    q_wide, q_thin = zip(*[q_rings(q_part, h) for h in range(2)])
    for h in range(2):
        q_part[h] = dot(grad[:, h * 512:(h + 1) * 512], docs, ROWS_CONTRACT).reshape(32, 16, 512)
        q_wide[h].start(FAR + NEAR)

    extra = extra + len(losses)
    for b, (c, j) in enumerate(blocks):
        d_part[c, j * 8:(j + 1) * 8] = dot(grads[b], queries).reshape(8, 16, 512)
    swap = remote(d_part.at[other['core']], pair, sems, extra, other)
    swap.start()
    docs_sum = Ring(at, 'z', d_part.at[core], 0, 8, d_buf, 0, sems, 4)
    q_wide[0].rs_pass()
    swap.wait_recv()
    add_into(d_part.at[core], 0, [(pair, 0)], 32)
    docs_sum.start(FAR + NEAR)
    q_wide[1].rs_pass()
    for wide, thin in zip(q_wide, q_thin):
        wide.rs_end()
        thin.start(FAR + NEAR)
    docs_sum.rs_pass()
    for ring in q_thin:
        ring.rs_pass()
    for c in losses:
        c.wait_recv()
    loss_ref[...] = sum(loss_all[j] for j in range(8)) / 8192.0
    for h, ring in enumerate(q_thin):
        ring.rs_end()
        q_up[h * 32:(h + 1) * 32, :] = q_part[h, pl.ds(own[h], 2)].reshape(32, 512).astype(BF16)
    docs_sum.rs_end()
    d_up[...] = d_part[core, pl.ds(z * 8, 8)].reshape(128, 512).astype(BF16)
    for c in shares + losses + [swap] + list(map(hand, range(SIDE))):
        c.wait_send()
    for ring in (*q_wide, *q_thin, docs_sum):
        ring.sent(FAR + NEAR + ON)
    for h in range(2):
        for ring in q_rings(q_all, h):
            ring.sent(GATHER)
    docs_ring.sent(GATHER)


def scores(tau, q_reps, d_reps):
    vmem = pl.BlockSpec(memory_space=pltpu.VMEM)
    copies = 5 * len(MESSAGES) + 27
    return pl.pallas_call(
        score_kernel,
        out_shape=tuple(jax.ShapeDtypeStruct(*s) for s in (((64, 512), BF16), ((128, 512), BF16), ((8, 128), F32))),
        in_specs=[pl.BlockSpec(memory_space=pltpu.SMEM), vmem, vmem],
        out_specs=(vmem,) * 3,
        scratch_shapes=[
            pltpu.VMEM((2, 32, 16, 512), BF16),
            pltpu.VMEM((2, 32, 16, 512), BF16),
            pltpu.VMEM((8, 128, 1024), F32),
            pltpu.VMEM((16, 3, 1024), F32),
            pltpu.VMEM((2, 32, 16, 512), F32),
            pltpu.VMEM((2, 32, 16, 512), F32),
            pltpu.VMEM((2, 30, 16, 512), F32),
            pltpu.VMEM((24, 16, 512), F32),
            pltpu.VMEM((32, 16, 512), F32),
            pltpu.VMEM((8, 8, 128), F32),
            pltpu.SemaphoreType.DMA((copies,)),
            pltpu.SemaphoreType.DMA((copies,)),
        ],
        compiler_params=pltpu.CompilerParams(collective_id=0, has_side_effects=True, vmem_limit_bytes=VMEM_LIMIT),
        name='scores',
    )(tau, q_reps, d_reps)


def gelu_back(pre, act_grad):
    return jax.vjp(jax.nn.gelu, pre)[1](act_grad)[0]


def tower_backward(sub, rows_per, x_ref, up_ref, w_one, w_two, w_proj, acc, pre_s, act_s):
    rows = pl.ds(pl.multiple_of(sub * rows_per, rows_per), rows_per)
    hidden = [x_ref[rows, :]]
    for layer in range(2):
        pre = dot(hidden[layer], w_one[layer])
        pre_s[layer, 0:rows_per] = pre
        act = jax.nn.gelu(pre).astype(BF16)
        act_s[layer, 0:rows_per] = act
        hidden.append((hidden[layer].astype(F32) + dot(act, w_two[layer])).astype(BF16))
    up = up_ref[rows, :]

    def add(base, stride, lhs, rhs):
        for i in range(lhs.shape[1] // 256):
            part = dot(lhs[:, i * 256:(i + 1) * 256], rhs, ROWS_CONTRACT)
            for j in range(2):
                spot = base + j * stride + i * 32
                acc[spot:spot + 32] += part[:, j * 256:(j + 1) * 256].reshape(32, 8, 256)

    add(2048, 64, hidden[2], up)
    resid = dot(up, w_proj[...], LAST_CONTRACT)
    for layer in (1, 0):
        resid_bf = resid.astype(BF16)
        add(1024 + layer * 512, 256, act_s[layer, 0:rows_per], resid_bf)
        act_grad = dot(resid_bf, w_two[layer], LAST_CONTRACT)
        pre_grad = gelu_back(pre_s[layer, 0:rows_per], act_grad).astype(BF16)
        for c in range(4):
            add(layer * 512 + c * 128, 64, hidden[layer], pre_grad[:, c * 512:(c + 1) * 512])
        if layer == 1:
            resid = resid + dot(pre_grad, w_one[layer], LAST_CONTRACT)


class Exchange:
    def __init__(self, acc, pair, bufs, sems):
        self.acc, self.pair = acc, pair
        self.pair_sems, self.ring_sems, self.hand_sems, self.credit, self.ready = sems[:2], sems[2:4], sems[4:6], sems[6], sems[7]
        self.at = place()
        self.core = self.at['core']
        self.other = moved(self.at, 'core', 1)
        self.around = [moved(self.at, d, s) for d in 'xyz' for s in (LEFT, RIGHT)]
        greet([self.other] + self.around)
        self.rings = {}
        for t in (Q, D):
            for k, (first, rows, dims) in enumerate(COLOURS):
                base = self.core * HALF + first
                for p in (OUTER, MIDDLE, INNER):
                    n = rows * RING_SIZE[p]
                    index = (t * len(COLOURS) + k) * len(RING_SIZE) + p
                    self.rings[t, k, p] = Ring(self.at, dims[p], acc.at[t], base, n, bufs[p], 3 * first // SIDE ** (p + 1), self.ring_sems, index)
                    base = base + self.at[dims[p]] * n

    def met(self):
        pl.semaphore_wait(pltpu.get_barrier_semaphore(), len(self.around) + 1)

    def level(self, t, p):
        return [self.rings[t, k, p] for k in range(len(COLOURS))]

    def pair_copy(self, t, rel, k):
        first, ring = COLOURS[k][0], self.rings[t, k, OUTER]
        spot = ring.spot[rel] + (1 - self.core * 2) * HALF
        dst = self.pair.at[PAIR_SLOT[rel], pl.ds(first // SIDE, ring.n)]
        return remote(self.acc.at[t, pl.ds(spot, ring.n)], dst, self.pair_sems, t * 12 + rel * 3 + k, self.other)

    def pairs(self, t, rel, fresh=False):
        if not fresh:
            pl.semaphore_wait(self.credit.at[PAIR_SLOT[rel]], 1)
        for k in range(len(COLOURS)):
            self.pair_copy(t, rel, k).start()

    def settle(self, t, rel, last=False):
        for k, ring in enumerate(self.level(t, OUTER)):
            self.pair_copy(t, rel, k).wait_recv()
            add_into(ring.x, ring.spot[rel], [(self.pair.at[PAIR_SLOT[rel]], COLOURS[k][0] // SIDE)], ring.n)
        if not last:
            pl.semaphore_signal(self.credit.at[PAIR_SLOT[rel]], inc=1, device_id=device(self.other), device_id_type=MESH)

    def start(self, t, p, which):
        for ring in self.level(t, p):
            ring.start(which)

    def rs_pass(self, t, p):
        for ring in self.level(t, p):
            ring.rs_pass()

    def rs_end(self, t, p):
        for ring in self.level(t, p):
            ring.rs_end()
        for k, ring in enumerate(self.level(t, p)):
            ring.sent(FAR + NEAR + ON)
            for rel in range(SIDE) if p == OUTER else ():
                self.pair_copy(t, rel, k).wait_send()
        for peer in self.around:
            pl.semaphore_signal(self.ready.at[t * 3 + p], inc=1, device_id=device(peer), device_id_type=MESH)
        if p == OUTER:
            pl.semaphore_signal(self.ready.at[6 + t], inc=1, device_id=device(self.other), device_id_type=MESH)

    def opened(self, t, p):
        pl.semaphore_wait(self.ready.at[t * 3 + p], len(self.around))

    def hand(self, t, k, p, rel, second):
        ring = self.rings[t, k, p]
        shift, size = (0, ring.n) if rel != ACROSS else (ring.half, ring.rest) if second else (0, ring.half)
        here = self.acc.at[t, pl.ds(ring.spot[rel] + shift, size)]
        kind = HANDS.index((rel, second))
        return remote(here, here, self.hand_sems, ((t * 3 + k) * 3 + p) * len(HANDS) + kind, self.other)

    def ag_start(self, t, p, which=FIRST + SECOND):
        self.start(t, p, which)
        if p == INNER:
            pl.semaphore_wait(self.ready.at[6 + t], 1)
            for k in range(len(COLOURS)):
                self.hand(t, k, p, OWN, False).start()

    def ag_pass(self, t, p):
        for ring in self.level(t, p):
            ring.ag_pass()
        for k, ring in enumerate(self.level(t, p)):
            for m, rel in zip(SECOND, (LEFT, RIGHT)):
                ring.take((m,))
                self.hand(t, k, p, rel, False).start()

    def ag_end(self, t, p):
        for k, ring in enumerate(self.level(t, p)):
            for m, second in zip(ONWARD, (False, True)):
                ring.take((m,))
                self.hand(t, k, p, ACROSS, second).start()

    def finish(self):
        hands = [(t, k, p, *h) for t, k, p in self.rings for h in HANDS if h[0] != OWN or p == INNER]
        for h in hands:
            self.hand(*h).wait_recv()
        for ring in self.rings.values():
            ring.sent(GATHER)
        for h in hands:
            self.hand(*h).wait_send()


def train_kernel(q_in, d_in, q_up, d_up, q_w1, q_w2, q_proj, d_w1, d_w2, d_proj, acc, w_one, w_two, w_proj, pre_s, act_s, pair, *rest):
    bufs, w_sems, sems = rest[:3], rest[3], rest[4:]
    ex = Exchange(acc, pair, bufs, sems)

    def load(refs):
        return [pltpu.make_async_copy(src, dst, w_sems.at[i]) for i, (src, dst) in enumerate(zip(refs, (w_one, w_two, w_proj)))]

    def clear(t):
        def body(i, carry):
            acc[t, pl.ds(i * 16, 16)] = jnp.zeros((16, 8, 256), F32)
            return carry

        lax.fori_loop(0, UNITS // 16, body, 0)

    loads = load((q_w1, q_w2, q_proj))
    for c in loads:
        c.start()
    clear(Q)
    for c in loads:
        c.wait()

    def q_body(sub, carry):
        tower_backward(sub, 16, q_in, q_up, w_one, w_two, w_proj, acc.at[Q], pre_s, act_s)
        return carry

    lax.fori_loop(0, SUB_COUNT, q_body, 0)
    ex.met()
    ex.pairs(Q, ACROSS, fresh=True)
    ex.pairs(Q, RIGHT, fresh=True)
    loads = load((d_w1, d_w2, d_proj))
    for c in loads:
        c.start()
    clear(D)
    ex.settle(Q, ACROSS)
    ex.start(Q, OUTER, FAR)
    ex.pairs(Q, LEFT)
    ex.settle(Q, RIGHT)
    ex.pairs(Q, OWN)
    for c in loads:
        c.wait()

    def d_body(sub, carry):
        tower_backward(sub, 32, d_in, d_up, w_one, w_two, w_proj, acc.at[D], pre_s, act_s)

        @pl.when(sub == 0)
        def _():
            ex.settle(Q, LEFT)
            ex.start(Q, OUTER, NEAR)
            ex.settle(Q, OWN)

        @pl.when(sub == 1)
        def _():
            ex.rs_pass(Q, OUTER)

        return carry

    lax.fori_loop(0, SUB_COUNT, d_body, 0)
    ex.pairs(D, ACROSS)
    ex.pairs(D, RIGHT)
    ex.rs_end(Q, OUTER)
    ex.start(Q, MIDDLE, FAR + NEAR)
    ex.settle(D, ACROSS)
    ex.pairs(D, LEFT)
    ex.rs_pass(Q, MIDDLE)
    ex.settle(D, RIGHT)
    ex.pairs(D, OWN)
    ex.rs_end(Q, MIDDLE)
    ex.start(Q, INNER, FAR + NEAR)
    ex.opened(Q, OUTER)
    ex.start(D, OUTER, FAR)
    ex.settle(D, LEFT, last=True)
    ex.rs_pass(Q, INNER)
    ex.start(D, OUTER, NEAR)
    ex.settle(D, OWN, last=True)
    ex.rs_end(Q, INNER)
    ex.opened(Q, INNER)
    ex.ag_start(Q, INNER)
    ex.rs_pass(D, OUTER)
    ex.ag_pass(Q, INNER)
    ex.ag_end(Q, INNER)
    ex.opened(Q, MIDDLE)
    ex.ag_start(Q, MIDDLE)
    ex.ag_pass(Q, MIDDLE)
    ex.rs_end(D, OUTER)
    ex.start(D, MIDDLE, FAR + NEAR)
    ex.ag_end(Q, MIDDLE)
    ex.ag_start(Q, OUTER, FIRST)
    ex.rs_pass(D, MIDDLE)
    ex.rs_end(D, MIDDLE)
    ex.start(D, INNER, FAR + NEAR)
    ex.ag_start(Q, OUTER, SECOND)
    ex.rs_pass(D, INNER)
    ex.rs_end(D, INNER)
    ex.opened(D, INNER)
    ex.ag_start(D, INNER)
    ex.ag_pass(Q, OUTER)
    ex.ag_pass(D, INNER)
    ex.ag_end(D, INNER)
    ex.opened(D, MIDDLE)
    ex.ag_start(D, MIDDLE)
    ex.ag_end(Q, OUTER)
    ex.ag_pass(D, MIDDLE)
    ex.ag_end(D, MIDDLE)
    ex.opened(D, OUTER)
    ex.ag_start(D, OUTER)
    ex.ag_pass(D, OUTER)
    ex.ag_end(D, OUTER)
    ex.finish()


def train(q_rows, d_rows, q_up, d_up, weights):
    vmem, whole = pl.BlockSpec(memory_space=pltpu.VMEM), pl.BlockSpec(memory_space=pl.ANY)
    bufs = [pltpu.VMEM((3 * HALF // SIDE ** p // SIDE, 8, 256), F32) for p in (OUTER, MIDDLE, INNER)]
    dma = pltpu.SemaphoreType.DMA
    return pl.pallas_call(
        train_kernel,
        out_shape=pltpu.VMEM((2, UNITS, 8, 256), F32),
        in_specs=[vmem] * 4 + [whole] * 6,
        out_specs=vmem,
        scratch_shapes=[
            pltpu.VMEM((2, 512, 2048), BF16),
            pltpu.VMEM((2, 2048, 512), BF16),
            pltpu.VMEM((512, 512), BF16),
            pltpu.VMEM((2, 32, 2048), F32),
            pltpu.VMEM((2, 32, 2048), BF16),
            pltpu.VMEM((2, 272, 8, 256), F32),
            *bufs,
            dma((3,)), *[dma((n,)) for n in (24, 24, 216, 216, 90, 90)],
            pltpu.SemaphoreType.REGULAR((2,)), pltpu.SemaphoreType.REGULAR((8,)),
        ],
        compiler_params=pltpu.CompilerParams(collective_id=1, has_side_effects=True, vmem_limit_bytes=TRAIN_VMEM),
        name='towers_backward_all_reduce',
    )(q_rows, d_rows, q_up, d_up, *weights)


def unpack_kernel(acc, *rest):
    outs, sem = rest[:6], rest[6]
    copies = []
    for t in range(2):
        one, two, proj = outs[t * 3:t * 3 + 3]
        for k in range(2):
            for c in range(8):
                copies.append((acc.at[t, pl.ds(k * 512 + c * 64, 64)], one.at[k, :, :, pl.ds(c * 256, 256)]))
            for c in range(2):
                copies.append((acc.at[t, pl.ds(1024 + k * 512 + c * 256, 256)], two.at[k, :, :, pl.ds(c * 256, 256)]))
        for c in range(2):
            copies.append((acc.at[t, pl.ds(2048 + c * 64, 64)], proj.at[:, :, pl.ds(c * 256, 256)]))
    copies = [pltpu.make_async_copy(src, dst, sem.at[i]) for i, (src, dst) in enumerate(copies)]
    for c in copies:
        c.start()
    for c in copies:
        c.wait()


def unpack(acc):
    shapes = ((2, 64, 8, 2048), (2, 256, 8, 512), (64, 8, 512)) * 2
    outs = pl.pallas_call(
        unpack_kernel,
        out_shape=tuple(jax.ShapeDtypeStruct(s, F32) for s in shapes),
        in_specs=[pl.BlockSpec(memory_space=pltpu.VMEM)],
        out_specs=(pl.BlockSpec(memory_space=pl.ANY),) * 6,
        scratch_shapes=[pltpu.SemaphoreType.DMA((44,))],
        compiler_params=pltpu.CompilerParams(vmem_limit_bytes=1 << 20),
        name='unpack',
    )(acc)
    final = ((2, 512, 2048), (2, 2048, 512), (512, 512)) * 2
    return tuple(o.reshape(s) for o, s in zip(outs, final))


def local_step(q_loc, d_loc, temperature, *weights):
    d_rows = d_loc.reshape(-1, d_loc.shape[-1])
    q_reps, d_reps = forward(q_loc, d_rows, weights)
    q_up, d_up, loss = scores(temperature.reshape(1), q_reps, d_reps)
    return (loss[0, 0], *unpack(train(q_loc, d_rows, q_up, d_up, weights)))


def solution(mesh):
    specs_in = (P('data', None), P(None, 'data', None), P(), P(), P(), P(), P(), P(), P())
    specs_out = (P(), P(), P(), P(), P(), P(), P())
    return jax.shard_map(local_step, mesh=mesh, in_specs=specs_in, out_specs=specs_out, check_vma=False)
```

time: 1330 us -> 277 us (0.21)
  waiting for transfers between devices: 807 us -> 0 us
  Pallas kernels: 0 us -> 274 us
  matrix products: 269 us -> 0 us
  other arithmetic: 124 us -> 0 us
  blocking collectives: 70.8 us -> 0 us
  local copies, waits for them, and re-layouts: 37.7 us -> 1.19 us
  between operations: 16.4 us -> 1.46 us
    reduce_scatter x1 -> x0, waiting for transfers between devices: 530 us -> none  [local_step(): lax.psum_scatter(doc_part.reshape(2, global_batch, rep_width), 'data', sc...]
    pallas_call x0 -> x4, Pallas kernels: none -> 274 us  [the longest x1 192 us: train(): pl.pallas_call(train_kernel, out_shape=pltpu.VMEM((2, UNITS, 8, 256), F32...]
    dot_general x115 -> x0, matrix products: 269 us -> none  [the longest x24 50 us: tower_forward(): pre_act = jnp.dot(hidden, w_one[layer], preferred_element_type=jnp.float32)]
    psum x1 -> x0, waiting for transfers between devices: 222 us -> none  [local_step(): q_one, q_two, q_pgrad = lax.psum(q_grads, 'data')]
    add x17 -> x0, other arithmetic: 118 us -> none  [the longest x16 118 us: body(): old_sum + new_part]
    psum x1 -> x0, blocking collectives: 70.8 us -> none  [local_step(): loss = lax.psum(jnp.sum(log_norm - pos_logit), 'data') / global_batch]
    all_gather x1 -> x0, waiting for transfers between devices: 55.2 us -> none  [local_step(): all_docs = lax.all_gather(d_reps, 'data', axis=1, tiled=True)]
    unnamed x30 -> x0, local copies, waits for them, and re-layouts: 25.9 us -> none
  transfers between devices with their start and end apart: 3 -> 0, of which waited for: 3 -> 0; matrix products, arithmetic and copies ran while one was open for 14% -> 0% of each run, Pallas kernels for 0% -> 0%
where the time goes in v2:
time: 277 us
  Pallas kernels  274 us (99%)
    pallas_call x1, Pallas kernels, train(): pl.pallas_call(train_kernel, out_shape=pltpu.VMEM((2, UNITS, 8, 256), F32...  192 us
    pallas_call x1, Pallas kernels, scores(): pl.pallas_call(score_kernel, out_shape=tuple((jax.ShapeDtypeStruct(*s) fo...  51.5 us
    pallas_call x1, Pallas kernels, forward(): pl.pallas_call(forward_kernel, out_shape=(jax.ShapeDtypeStruct(q_rows.sha...  19.3 us
    pallas_call x1, Pallas kernels, unpack(): pl.pallas_call(unpack_kernel, out_shape=tuple((jax.ShapeDtypeStruct(s, F3...  11.9 us

profile of v2, /device:TPU:1, one launch (start us, length us, event | category | flops | bytes accessed | tf_op | source)
XLA Modules:
  0.0 276.9 jit_solution(2801859791053949210)
XLA Ops:
  1.3 19.3 %towers_forward.1 = (bf16[64,512]{1,0:T(8,128)(2,1)}, bf16[128,512]{1,0:T(8,128)(2,1)}) custom-call(bf16[64,512]{1,0:T(8,128)(2,1)} %q_in.3, bf16[128,512]{1,0:T(8,128)(2,1)} %bitcast.10, bf16[2,512,2048]{2,1,0:T(8,128)(2,1)} %q_w1.3, bf16[2,2048,512]{2,1,0:T(8,128)(2,1)} %q_w2.3, bf16[512,512]{1,0:T(8,128)(2,1)} %q_proj.3, bf16[2,512,2048]{2,1,0:T(8,128)(2,1)} %d_w1.3, ...), custom_call_target="tpu_custom_call" | custom-call | tf_op jit(solution)/shard_map/towers_forward/pallas_call | solution.py:155
  20.6 51.5 %scores.1 = (bf16[64,512]{1,0:T(8,128)(2,1)}, bf16[128,512]{1,0:T(8,128)(2,1)}, f32[8,128]{1,0:T(8,128)}) custom-call(f32[1]{0:T(128)} %bitcast.9.tau_ref, bf16[64,512]{1,0:T(8,128)(2,1)} %get-tuple-element.18.q_ref, bf16[128,512]{1,0:T(8,128)(2,1)} %get-tuple-element.19.d_ref), custom_call_target="tpu_custom_call" | custom-call | tf_op jit(solution)/shard_map/scores/pallas_call | solution.py:306
  72.0 1.2 slice.3
  73.2 191.7 %towers_backward_all_reduce.1.acc = f32[2,2176,8,256]{3,2,1,0:T(8,128)S(1)} custom-call(bf16[64,512]{1,0:T(8,128)(2,1)} %q_in.3, bf16[128,512]{1,0:T(8,128)(2,1)} %bitcast.11, bf16[64,512]{1,0:T(8,128)(2,1)} %get-tuple-element.21.q_up, bf16[128,512]{1,0:T(8,128)(2,1)} %get-tuple-element.22.d_up, bf16[2,512,2048]{2,1,0:T(8,128)(2,1)} %q_w1.3, ...), custom_call_target="tpu_custom_call" | custom-call | tf_op jit(solution)/shard_map/towers_backward_all_reduce/pallas_call | solution.py:584
  264.9 11.9 %unpack.1 = (f32[2,64,8,2048]{3,2,1,0:T(8,128)}, f32[2,256,8,512]{3,2,1,0:T(8,128)}, f32[64,8,512]{2,1,0:T(8,128)}, f32[2,64,8,2048]{3,2,1,0:T(8,128)}, f32[2,25...) custom-call(f32[2,2176,8,256]{3,2,1,0:T(8,128)S(1)} %towers_backward_all_reduce.1.acc), custom_call_target="tpu_custom_call" | custom-call | tf_op jit(solution)/shard_map/unpack/pallas_call | solution.py:626

commit v3 on v2

--- a/solution.py
+++ b/solution.py
@@ -31,6 +31,8 @@
 ALL = tuple(range(len(MESSAGES)))
 FAR, NEAR, ON, GATHER = ALL[:2], ALL[2:4], ALL[4:6], ALL[6:]
 FIRST, SECOND, ONWARD = GATHER[:2], GATHER[2:4], GATHER[4:]
+DIM, FFN, COLS = 512, 2048, 256
+WEIGHT_SHAPES = ((2, DIM, FFN), (2, FFN, DIM), (DIM, DIM))
 COLOURS = ((0, 6, ('x', 'y', 'z')), (384, 6, ('y', 'z', 'x')), (768, 5, ('z', 'x', 'y')))
 HANDS = ((LEFT, False), (RIGHT, False), (ACROSS, False), (ACROSS, True), (OWN, False))
 
@@ -131,38 +133,31 @@
             self.copy(then).start()
 
 
-def tower_forward(rows, w_one, w_two, w_proj):
+def tower_forward(rows, w_one, w_two, w_proj, ready):
     hidden = rows
     for layer in range(2):
+        ready(2 * layer)
         act = jax.nn.gelu(dot(hidden, w_one[layer])).astype(BF16)
+        ready(2 * layer + 1)
         hidden = (hidden.astype(F32) + dot(act, w_two[layer])).astype(BF16)
+    ready(4)
     return dot(hidden, w_proj[...]).astype(BF16)
 
 
-def forward_kernel(q_in, d_in, q_w1, q_w2, q_proj, d_w1, d_w2, d_proj, q_out, d_out):
-    def body(sub, carry):
-        rows = pl.ds(pl.multiple_of(sub * 16, 16), 16)
-        q_out[rows, :] = tower_forward(q_in[rows, :], q_w1, q_w2, q_proj)
-        rows = pl.ds(pl.multiple_of(sub * 32, 32), 32)
-        d_out[rows, :] = tower_forward(d_in[rows, :], d_w1, d_w2, d_proj)
-        return carry
-
-    lax.fori_loop(0, SUB_COUNT, body, 0)
-
-
-def forward(q_rows, d_rows, weights):
-    vmem = pl.BlockSpec(memory_space=pltpu.VMEM)
-    return pl.pallas_call(
-        forward_kernel,
-        out_shape=(jax.ShapeDtypeStruct(q_rows.shape, BF16), jax.ShapeDtypeStruct(d_rows.shape, BF16)),
-        in_specs=[vmem] * 8,
-        out_specs=(vmem, vmem),
-        compiler_params=pltpu.CompilerParams(vmem_limit_bytes=VMEM_LIMIT),
-        name='towers_forward',
-    )(q_rows, d_rows, *weights)
-
-
-def score_kernel(tau_ref, q_ref, d_ref, q_up, d_up, loss_ref, q_all, d_all, st, stats, q_part, d_part, q_buf, d_buf, pair, loss_all, *sems):
+def weight_loads(src, dst, sems, at=0):
+    pairs = [(one.at[layer], two.at[layer]) for layer in range(2) for one, two in zip(src[:2], dst[:2])]
+    return [pltpu.make_async_copy(one, two, sems.at[at + i]) for i, (one, two) in enumerate(pairs + [(src[2], dst[2])])]
+
+
+def score_kernel(
+    tau_ref, q_ref, d_ref, q_w1, q_w2, q_proj, d_w1, d_w2, d_proj, q_up, d_up, loss_ref,
+    q_all, d_all, st, stats, q_part, d_part, q_buf, d_buf, pair, loss_all, q_one, q_two, q_last, d_one, d_two, d_last, w_sems, *sems
+):
+    q_weights, d_weights = (q_one, q_two, q_last), (d_one, d_two, d_last)
+    q_loads = weight_loads((q_w1, q_w2, q_proj), q_weights, w_sems)
+    d_loads = weight_loads((d_w1, d_w2, d_proj), d_weights, w_sems, len(q_loads))
+    for c in q_loads + d_loads:
+        c.start()
     at = place()
     core, z = at['core'], at['z']
     other = moved(at, 'core', 1)
@@ -173,9 +168,6 @@
 
     outer, inner = ('y', 'x'), ('x', 'y')
     own = [at[outer[h]] * 8 + at[inner[h]] * 2 for h in range(2)]
-    for h in range(2):
-        q_all[h, pl.ds(own[h], 2)] = q_ref[h * 32:(h + 1) * 32, :].reshape(2, 16, 512)
-    d_all[core, pl.ds(z * 8, 8)] = d_ref[...].reshape(8, 16, 512)
 
     def q_rings(x, h):
         wide = Ring(at, outer[h], x.at[h], 0, 8, q_buf.at[h], 0, sems, h)
@@ -184,40 +176,67 @@
     q_wide, q_thin = zip(*[q_rings(q_all, h) for h in range(2)])
     docs_ring = Ring(at, 'z', d_all.at[core], 0, 8, d_buf, 0, sems, 4)
     hands_at = 5 * len(MESSAGES)
-    pl.semaphore_wait(pltpu.get_barrier_semaphore(), len(q_peers) + len(d_peers))
-
     def hand(rel):
         here = d_all.at[core, pl.ds(docs_ring.spot[rel], 8)]
         return remote(here, here, sems, hands_at + rel, other)
 
-    docs_ring.start(FIRST + SECOND)
+    for h in range(2):
+        def q_body(i, carry):
+            def ready(step):
+                if h == 0:
+                    pl.when(i == 0)(q_loads[step].wait)
+
+            rows = pl.ds(pl.multiple_of((h * 2 + i) * 16, 16), 16)
+            q_all[h, own[h] + i] = tower_forward(q_ref[rows, :], *q_weights, ready)
+            return carry
+
+        lax.fori_loop(0, 2, q_body, 0)
+        if h == 0:
+            pl.semaphore_wait(pltpu.get_barrier_semaphore(), len(q_peers) + len(d_peers))
+        q_thin[h].start(FIRST + SECOND)
+    for c in d_loads:
+        c.wait()
+
+    def d_body(i, carry):
+        rows = pl.ds(pl.multiple_of(i * 32, 32), 32)
+        d_all[core, pl.ds(z * 8 + i * 2, 2)] = tower_forward(d_ref[rows, :], *d_weights, lambda step: None).reshape(2, 16, DIM)
+
+        @pl.when(i == 0)
+        def _():
+            for ring in q_thin:
+                ring.ag_pass()
+
+        @pl.when(i == 1)
+        def _():
+            docs_ring.start(FIRST[:1] + SECOND[1:])
+            for thin, wide in zip(q_thin, q_wide):
+                thin.take(SECOND + ONWARD)
+                wide.start(FIRST + SECOND)
+
+        return carry
+
+    lax.fori_loop(0, SUB_COUNT, d_body, 0)
+    docs_ring.start(FIRST[1:] + SECOND[:1])
     hand(OWN).start()
-    for ring in q_thin:
-        ring.start(FIRST + SECOND)
-    for ring in q_thin:
+    for ring in q_wide:
         ring.ag_pass()
     docs_ring.ag_pass()
-    for thin, wide in zip(q_thin, q_wide):
-        thin.take(SECOND + ONWARD)
-        wide.start(FIRST + SECOND)
     docs_ring.take(SECOND)
     hand(LEFT).start()
     hand(RIGHT).start()
     docs_ring.take(ONWARD)
     hand(ACROSS).start()
     for ring in q_wide:
-        ring.ag_pass()
+        ring.take(SECOND + ONWARD)
     for rel in range(SIDE):
         hand(rel).wait_recv()
-    for ring in q_wide:
-        ring.take(SECOND + ONWARD)
 
     tau = tau_ref[0]
-    queries = q_all[...].reshape(1024, 512)
+    queries = q_all[...].reshape(1024, DIM)
     blocks = [(c, j) for c in range(2) for j in range(SIDE)]
 
     def block(ref, c, j):
-        return ref[c, j * 8:(j + 1) * 8].reshape(128, 512)
+        return ref[c, j * 8:(j + 1) * 8].reshape(128, DIM)
 
     highs = []
     for b, (c, j) in enumerate(blocks):
@@ -259,15 +278,15 @@
         soft = jnp.exp(st[b] - log_norm) - jnp.where(hit & (d_slot == b), 1.0, 0.0)
         grads.append((soft / scale).astype(BF16))
     grad = jnp.concatenate(grads, axis=0)
-    docs = d_all[...].reshape(1024, 512)
+    docs = d_all[...].reshape(1024, DIM)
     q_wide, q_thin = zip(*[q_rings(q_part, h) for h in range(2)])
     for h in range(2):
-        q_part[h] = dot(grad[:, h * 512:(h + 1) * 512], docs, ROWS_CONTRACT).reshape(32, 16, 512)
+        q_part[h] = dot(grad[:, h * DIM:(h + 1) * DIM], docs, ROWS_CONTRACT).reshape(32, 16, DIM)
         q_wide[h].start(FAR + NEAR)
 
     extra = extra + len(losses)
     for b, (c, j) in enumerate(blocks):
-        d_part[c, j * 8:(j + 1) * 8] = dot(grads[b], queries).reshape(8, 16, 512)
+        d_part[c, j * 8:(j + 1) * 8] = dot(grads[b], queries).reshape(8, 16, DIM)
     swap = remote(d_part.at[other['core']], pair, sems, extra, other)
     swap.start()
     docs_sum = Ring(at, 'z', d_part.at[core], 0, 8, d_buf, 0, sems, 4)
@@ -284,12 +303,12 @@
         ring.rs_pass()
     for c in losses:
         c.wait_recv()
-    loss_ref[...] = sum(loss_all[j] for j in range(8)) / 8192.0
+    loss_ref[...] = sum(loss_all[j, 0:1, 0:1] for j in range(8)) / 8192.0
     for h, ring in enumerate(q_thin):
         ring.rs_end()
-        q_up[h * 32:(h + 1) * 32, :] = q_part[h, pl.ds(own[h], 2)].reshape(32, 512).astype(BF16)
+        q_up[h * 32:(h + 1) * 32, :] = q_part[h, pl.ds(own[h], 2)].reshape(32, DIM).astype(BF16)
     docs_sum.rs_end()
-    d_up[...] = d_part[core, pl.ds(z * 8, 8)].reshape(128, 512).astype(BF16)
+    d_up[...] = d_part[core, pl.ds(z * 8, 8)].reshape(128, DIM).astype(BF16)
     for c in shares + losses + [swap] + list(map(hand, range(SIDE))):
         c.wait_send()
     for ring in (*q_wide, *q_thin, docs_sum):
@@ -300,38 +319,40 @@
     docs_ring.sent(GATHER)
 
 
-def scores(tau, q_reps, d_reps):
-    vmem = pl.BlockSpec(memory_space=pltpu.VMEM)
+def scores(tau, q_rows, d_rows, weights):
+    vmem, whole = pl.BlockSpec(memory_space=pltpu.VMEM), pl.BlockSpec(memory_space=pl.ANY)
     copies = 5 * len(MESSAGES) + 27
     return pl.pallas_call(
         score_kernel,
-        out_shape=tuple(jax.ShapeDtypeStruct(*s) for s in (((64, 512), BF16), ((128, 512), BF16), ((8, 128), F32))),
-        in_specs=[pl.BlockSpec(memory_space=pltpu.SMEM), vmem, vmem],
+        out_shape=tuple(jax.ShapeDtypeStruct(*s) for s in (((64, DIM), BF16), ((128, DIM), BF16), ((1, 1), F32))),
+        in_specs=[pl.BlockSpec(memory_space=pltpu.SMEM), vmem, vmem] + [whole] * 6,
         out_specs=(vmem,) * 3,
         scratch_shapes=[
-            pltpu.VMEM((2, 32, 16, 512), BF16),
-            pltpu.VMEM((2, 32, 16, 512), BF16),
+            pltpu.VMEM((2, 32, 16, DIM), BF16),
+            pltpu.VMEM((2, 32, 16, DIM), BF16),
             pltpu.VMEM((8, 128, 1024), F32),
             pltpu.VMEM((16, 3, 1024), F32),
-            pltpu.VMEM((2, 32, 16, 512), F32),
-            pltpu.VMEM((2, 32, 16, 512), F32),
-            pltpu.VMEM((2, 30, 16, 512), F32),
-            pltpu.VMEM((24, 16, 512), F32),
-            pltpu.VMEM((32, 16, 512), F32),
+            pltpu.VMEM((2, 32, 16, DIM), F32),
+            pltpu.VMEM((2, 32, 16, DIM), F32),
+            pltpu.VMEM((2, 30, 16, DIM), F32),
+            pltpu.VMEM((24, 16, DIM), F32),
+            pltpu.VMEM((32, 16, DIM), F32),
             pltpu.VMEM((8, 8, 128), F32),
+            *[pltpu.VMEM(shape, BF16) for shape in WEIGHT_SHAPES * 2],
+            pltpu.SemaphoreType.DMA((10,)),
             pltpu.SemaphoreType.DMA((copies,)),
             pltpu.SemaphoreType.DMA((copies,)),
         ],
         compiler_params=pltpu.CompilerParams(collective_id=0, has_side_effects=True, vmem_limit_bytes=VMEM_LIMIT),
-        name='scores',
-    )(tau, q_reps, d_reps)
+        name='towers_forward_scores',
+    )(tau, q_rows, d_rows, *weights)
 
 
 def gelu_back(pre, act_grad):
     return jax.vjp(jax.nn.gelu, pre)[1](act_grad)[0]
 
 
-def tower_backward(sub, rows_per, x_ref, up_ref, w_one, w_two, w_proj, acc, pre_s, act_s):
+def tower_backward(sub, rows_per, x_ref, up_ref, w_one, w_two, w_proj, acc, pre_s, act_s, hook):
     rows = pl.ds(pl.multiple_of(sub * rows_per, rows_per), rows_per)
     hidden = [x_ref[rows, :]]
     for layer in range(2):
@@ -339,27 +360,32 @@
         pre_s[layer, 0:rows_per] = pre
         act = jax.nn.gelu(pre).astype(BF16)
         act_s[layer, 0:rows_per] = act
+        if layer == 0:
+            hook(0)
         hidden.append((hidden[layer].astype(F32) + dot(act, w_two[layer])).astype(BF16))
+    hook(1)
     up = up_ref[rows, :]
 
     def add(base, stride, lhs, rhs):
-        for i in range(lhs.shape[1] // 256):
-            part = dot(lhs[:, i * 256:(i + 1) * 256], rhs, ROWS_CONTRACT)
+        for i in range(lhs.shape[1] // COLS):
+            part = dot(lhs[:, i * COLS:(i + 1) * COLS], rhs, ROWS_CONTRACT)
             for j in range(2):
                 spot = base + j * stride + i * 32
-                acc[spot:spot + 32] += part[:, j * 256:(j + 1) * 256].reshape(32, 8, 256)
-
-    add(2048, 64, hidden[2], up)
+                acc[spot:spot + 32] += part[:, j * COLS:(j + 1) * COLS].reshape(32, 8, COLS)
+
+    add(FFN, 64, hidden[2], up)
     resid = dot(up, w_proj[...], LAST_CONTRACT)
     for layer in (1, 0):
         resid_bf = resid.astype(BF16)
-        add(1024 + layer * 512, 256, act_s[layer, 0:rows_per], resid_bf)
+        add(1024 + layer * DIM, COLS, act_s[layer, 0:rows_per], resid_bf)
         act_grad = dot(resid_bf, w_two[layer], LAST_CONTRACT)
         pre_grad = gelu_back(pre_s[layer, 0:rows_per], act_grad).astype(BF16)
         for c in range(4):
-            add(layer * 512 + c * 128, 64, hidden[layer], pre_grad[:, c * 512:(c + 1) * 512])
+            add(layer * DIM + c * 128, 64, hidden[layer], pre_grad[:, c * DIM:(c + 1) * DIM])
         if layer == 1:
             resid = resid + dot(pre_grad, w_one[layer], LAST_CONTRACT)
+            hook(2)
+    hook(3)
 
 
 class Exchange:
@@ -471,56 +497,72 @@
     bufs, w_sems, sems = rest[:3], rest[3], rest[4:]
     ex = Exchange(acc, pair, bufs, sems)
 
-    def load(refs):
-        return [pltpu.make_async_copy(src, dst, w_sems.at[i]) for i, (src, dst) in enumerate(zip(refs, (w_one, w_two, w_proj)))]
-
-    def clear(t):
-        def body(i, carry):
-            acc[t, pl.ds(i * 16, 16)] = jnp.zeros((16, 8, 256), F32)
-            return carry
-
-        lax.fori_loop(0, UNITS // 16, body, 0)
-
-    loads = load((q_w1, q_w2, q_proj))
-    for c in loads:
+    held = (w_one, w_two, w_proj)
+    q_loads, d_loads = weight_loads((q_w1, q_w2, q_proj), held, w_sems), weight_loads((d_w1, d_w2, d_proj), held, w_sems)
+    for c in q_loads:
         c.start()
-    clear(Q)
-    for c in loads:
+
+    def clear(i, carry):
+        for t in (Q, D):
+            acc[t, pl.ds(i * 16, 16)] = jnp.zeros((16, 8, COLS), F32)
+        return carry
+
+    lax.fori_loop(0, UNITS // 16, clear, 0)
+    for c in q_loads:
         c.wait()
 
+    def at_hooks(sub, table):
+        def hook(i):
+            for when, work in table:
+                if when[1] == i:
+                    pl.when(sub == when[0])(work)
+
+        return hook
+
+    def swap_early():
+        d_loads[0].start()
+
+    def swap_late():
+        for c in d_loads[2:]:
+            c.start()
+
     def q_body(sub, carry):
-        tower_backward(sub, 16, q_in, q_up, w_one, w_two, w_proj, acc.at[Q], pre_s, act_s)
+        hook = at_hooks(sub, (((3, 1), swap_early), ((3, 2), swap_late)))
+        tower_backward(sub, 16, q_in, q_up, *held, acc.at[Q], pre_s, act_s, hook)
         return carry
 
     lax.fori_loop(0, SUB_COUNT, q_body, 0)
+    d_loads[1].start()
     ex.met()
     ex.pairs(Q, ACROSS, fresh=True)
     ex.pairs(Q, RIGHT, fresh=True)
-    loads = load((d_w1, d_w2, d_proj))
-    for c in loads:
-        c.start()
-    clear(D)
-    ex.settle(Q, ACROSS)
-    ex.start(Q, OUTER, FAR)
-    ex.pairs(Q, LEFT)
-    ex.settle(Q, RIGHT)
-    ex.pairs(Q, OWN)
-    for c in loads:
+    d_loads[0].wait()
+    for c in d_loads[2:]:
         c.wait()
 
+    def across():
+        ex.settle(Q, ACROSS)
+        ex.start(Q, OUTER, FAR)
+
+    def right():
+        ex.pairs(Q, LEFT)
+        ex.settle(Q, RIGHT)
+
+    def left():
+        ex.settle(Q, LEFT)
+        ex.start(Q, OUTER, NEAR)
+
+    def own():
+        ex.settle(Q, OWN)
+        ex.rs_pass(Q, OUTER)
+
+    steps = (
+        ((0, 0), d_loads[1].wait), ((0, 2), across), ((0, 3), right),
+        ((1, 1), functools.partial(ex.pairs, Q, OWN)), ((1, 2), left), ((1, 3), own),
+    )
+
     def d_body(sub, carry):
-        tower_backward(sub, 32, d_in, d_up, w_one, w_two, w_proj, acc.at[D], pre_s, act_s)
-
-        @pl.when(sub == 0)
-        def _():
-            ex.settle(Q, LEFT)
-            ex.start(Q, OUTER, NEAR)
-            ex.settle(Q, OWN)
-
-        @pl.when(sub == 1)
-        def _():
-            ex.rs_pass(Q, OUTER)
-
+        tower_backward(sub, 32, d_in, d_up, *held, acc.at[D], pre_s, act_s, at_hooks(sub, steps))
         return carry
 
     lax.fori_loop(0, SUB_COUNT, d_body, 0)
@@ -531,44 +573,44 @@
     ex.settle(D, ACROSS)
     ex.pairs(D, LEFT)
     ex.rs_pass(Q, MIDDLE)
+    ex.opened(Q, OUTER)
+    ex.start(D, OUTER, FAR)
     ex.settle(D, RIGHT)
     ex.pairs(D, OWN)
     ex.rs_end(Q, MIDDLE)
     ex.start(Q, INNER, FAR + NEAR)
-    ex.opened(Q, OUTER)
-    ex.start(D, OUTER, FAR)
     ex.settle(D, LEFT, last=True)
-    ex.rs_pass(Q, INNER)
     ex.start(D, OUTER, NEAR)
     ex.settle(D, OWN, last=True)
+    ex.rs_pass(Q, INNER)
+    ex.rs_pass(D, OUTER)
     ex.rs_end(Q, INNER)
     ex.opened(Q, INNER)
     ex.ag_start(Q, INNER)
-    ex.rs_pass(D, OUTER)
+    ex.rs_end(D, OUTER)
+    ex.opened(Q, MIDDLE)
+    ex.start(D, MIDDLE, FAR + NEAR)
     ex.ag_pass(Q, INNER)
     ex.ag_end(Q, INNER)
-    ex.opened(Q, MIDDLE)
     ex.ag_start(Q, MIDDLE)
+    ex.rs_pass(D, MIDDLE)
     ex.ag_pass(Q, MIDDLE)
-    ex.rs_end(D, OUTER)
-    ex.start(D, MIDDLE, FAR + NEAR)
+    ex.rs_end(D, MIDDLE)
+    ex.start(D, INNER, FAR + NEAR)
     ex.ag_end(Q, MIDDLE)
     ex.ag_start(Q, OUTER, FIRST)
-    ex.rs_pass(D, MIDDLE)
-    ex.rs_end(D, MIDDLE)
-    ex.start(D, INNER, FAR + NEAR)
-    ex.ag_start(Q, OUTER, SECOND)
     ex.rs_pass(D, INNER)
     ex.rs_end(D, INNER)
     ex.opened(D, INNER)
     ex.ag_start(D, INNER)
+    ex.ag_start(Q, OUTER, SECOND)
+    ex.ag_pass(D, INNER)
     ex.ag_pass(Q, OUTER)
-    ex.ag_pass(D, INNER)
     ex.ag_end(D, INNER)
     ex.opened(D, MIDDLE)
     ex.ag_start(D, MIDDLE)
+    ex.ag_pass(D, MIDDLE)
     ex.ag_end(Q, OUTER)
-    ex.ag_pass(D, MIDDLE)
     ex.ag_end(D, MIDDLE)
     ex.opened(D, OUTER)
     ex.ag_start(D, OUTER)
@@ -579,22 +621,20 @@
 
 def train(q_rows, d_rows, q_up, d_up, weights):
     vmem, whole = pl.BlockSpec(memory_space=pltpu.VMEM), pl.BlockSpec(memory_space=pl.ANY)
-    bufs = [pltpu.VMEM((3 * HALF // SIDE ** p // SIDE, 8, 256), F32) for p in (OUTER, MIDDLE, INNER)]
+    bufs = [pltpu.VMEM((3 * HALF // SIDE ** p // SIDE, 8, COLS), F32) for p in (OUTER, MIDDLE, INNER)]
     dma = pltpu.SemaphoreType.DMA
     return pl.pallas_call(
         train_kernel,
-        out_shape=pltpu.VMEM((2, UNITS, 8, 256), F32),
+        out_shape=pltpu.VMEM((2, UNITS, 8, COLS), F32),
         in_specs=[vmem] * 4 + [whole] * 6,
         out_specs=vmem,
         scratch_shapes=[
-            pltpu.VMEM((2, 512, 2048), BF16),
-            pltpu.VMEM((2, 2048, 512), BF16),
-            pltpu.VMEM((512, 512), BF16),
-            pltpu.VMEM((2, 32, 2048), F32),
-            pltpu.VMEM((2, 32, 2048), BF16),
-            pltpu.VMEM((2, 272, 8, 256), F32),
+            *[pltpu.VMEM(shape, BF16) for shape in WEIGHT_SHAPES],
+            pltpu.VMEM((2, 32, FFN), F32),
+            pltpu.VMEM((2, 32, FFN), BF16),
+            pltpu.VMEM((2, 272, 8, COLS), F32),
             *bufs,
-            dma((3,)), *[dma((n,)) for n in (24, 24, 216, 216, 90, 90)],
+            dma((5,)), *[dma((n,)) for n in (24, 24, 216, 216, 90, 90)],
             pltpu.SemaphoreType.REGULAR((2,)), pltpu.SemaphoreType.REGULAR((8,)),
         ],
         compiler_params=pltpu.CompilerParams(collective_id=1, has_side_effects=True, vmem_limit_bytes=TRAIN_VMEM),
@@ -609,11 +649,11 @@
         one, two, proj = outs[t * 3:t * 3 + 3]
         for k in range(2):
             for c in range(8):
-                copies.append((acc.at[t, pl.ds(k * 512 + c * 64, 64)], one.at[k, :, :, pl.ds(c * 256, 256)]))
+                copies.append((acc.at[t, pl.ds(k * DIM + c * 64, 64)], one.at[k, :, :, pl.ds(c * COLS, COLS)]))
             for c in range(2):
-                copies.append((acc.at[t, pl.ds(1024 + k * 512 + c * 256, 256)], two.at[k, :, :, pl.ds(c * 256, 256)]))
+                copies.append((acc.at[t, pl.ds(1024 + k * DIM + c * COLS, COLS)], two.at[k, :, :, pl.ds(c * COLS, COLS)]))
         for c in range(2):
-            copies.append((acc.at[t, pl.ds(2048 + c * 64, 64)], proj.at[:, :, pl.ds(c * 256, 256)]))
+            copies.append((acc.at[t, pl.ds(FFN + c * 64, 64)], proj.at[:, :, pl.ds(c * COLS, COLS)]))
     copies = [pltpu.make_async_copy(src, dst, sem.at[i]) for i, (src, dst) in enumerate(copies)]
     for c in copies:
         c.start()
@@ -622,7 +662,7 @@
 
 
 def unpack(acc):
-    shapes = ((2, 64, 8, 2048), (2, 256, 8, 512), (64, 8, 512)) * 2
+    shapes = ((2, 64, 8, FFN), (2, COLS, 8, DIM), (64, 8, DIM)) * 2
     outs = pl.pallas_call(
         unpack_kernel,
         out_shape=tuple(jax.ShapeDtypeStruct(s, F32) for s in shapes),
@@ -632,15 +672,13 @@
         compiler_params=pltpu.CompilerParams(vmem_limit_bytes=1 << 20),
         name='unpack',
     )(acc)
-    final = ((2, 512, 2048), (2, 2048, 512), (512, 512)) * 2
-    return tuple(o.reshape(s) for o, s in zip(outs, final))
+    return tuple(o.reshape(s) for o, s in zip(outs, WEIGHT_SHAPES * 2))
 
 
 def local_step(q_loc, d_loc, temperature, *weights):
     d_rows = d_loc.reshape(-1, d_loc.shape[-1])
-    q_reps, d_reps = forward(q_loc, d_rows, weights)
-    q_up, d_up, loss = scores(temperature.reshape(1), q_reps, d_reps)
-    return (loss[0, 0], *unpack(train(q_loc, d_rows, q_up, d_up, weights)))
+    q_up, d_up, loss = scores(temperature.reshape(1), q_loc, d_rows, weights)
+    return (loss.reshape(()), *unpack(train(q_loc, d_rows, q_up, d_up, weights)))
 
 
 def solution(mesh):

time: 277 us -> 261 us (0.942)
  Pallas kernels: 274 us -> 258 us
    pallas_call x2 -> x1, Pallas kernels: 211 us -> 184 us  [train(): pl.pallas_call(train_kernel, out_shape=pltpu.VMEM((2, UNITS, 8, COLS), F3...]
    pallas_call x1, Pallas kernels: 51.5 us -> 62.2 us  [scores(): pl.pallas_call(score_kernel, out_shape=tuple((jax.ShapeDtypeStruct(*s) fo...]
where the time goes in v3:
time: 261 us
  Pallas kernels  258 us (99%)
  between operations  2.99 us (1%)
    pallas_call x1, Pallas kernels, train(): pl.pallas_call(train_kernel, out_shape=pltpu.VMEM((2, UNITS, 8, COLS), F3...  184 us
    pallas_call x1, Pallas kernels, scores(): pl.pallas_call(score_kernel, out_shape=tuple((jax.ShapeDtypeStruct(*s) fo...  62.2 us
    pallas_call x1, Pallas kernels, unpack(): pl.pallas_call(unpack_kernel, out_shape=tuple((jax.ShapeDtypeStruct(s, F3...  11.9 us

profile of v3, /device:TPU:1, one launch (start us, length us, event | category | flops | bytes accessed | tf_op | source)
XLA Modules:
  0.0 261.3 jit_solution(724519181651713160)
XLA Ops:
  1.3 62.2 %towers_forward_scores.1 = (bf16[64,512]{1,0:T(8,128)(2,1)}, bf16[128,512]{1,0:T(8,128)(2,1)}, f32[1,1]{1,0:T(1,128)}) custom-call(f32[1]{0:T(128)} %bitcast.9.tau_ref, bf16[64,512]{1,0:T(8,128)(2,1)} %q_in.1, bf16[128,512]{1,0:T(8,128)(2,1)} %bitcast.10, bf16[2,512,2048]{2,1,0:T(8,128)(2,1)} %q_w1.3, bf16[2,2048,512]{2,1,0:T(8,128)(2,1)} %q_w2.3, ...), custom_call_target="tpu_custom_call" | custom-call | tf_op jit(solution)/shard_map/towers_forward_scores/pallas_call | solution.py:325
  63.5 184.3 %towers_backward_all_reduce.1.acc = f32[2,2176,8,256]{3,2,1,0:T(8,128)S(1)} custom-call(bf16[64,512]{1,0:T(8,128)(2,1)} %q_in.1, bf16[128,512]{1,0:T(8,128)(2,1)} %bitcast.11, bf16[64,512]{1,0:T(8,128)(2,1)} %get-tuple-element.17.q_up, bf16[128,512]{1,0:T(8,128)(2,1)} %get-tuple-element.18.d_up, bf16[2,512,2048]{2,1,0:T(8,128)(2,1)} %q_w1.3, ...), custom_call_target="tpu_custom_call" | custom-call | tf_op jit(solution)/shard_map/towers_backward_all_reduce/pallas_call | solution.py:626
  247.7 11.9 %unpack.1 = (f32[2,64,8,2048]{3,2,1,0:T(8,128)}, f32[2,256,8,512]{3,2,1,0:T(8,128)}, f32[64,8,512]{2,1,0:T(8,128)}, f32[2,64,8,2048]{3,2,1,0:T(8,128)}, f32[2,25...) custom-call(f32[2,2176,8,256]{3,2,1,0:T(8,128)S(1)} %towers_backward_all_reduce.1.acc), custom_call_target="tpu_custom_call" | custom-call | tf_op jit(solution)/shard_map/unpack/pallas_call | solution.py:666

commit v4 on v3

--- a/solution.py
+++ b/solution.py
@@ -14,7 +14,7 @@
 SIDE = 4
 ROWS_CONTRACT = (((0,), (0,)), ((), ()))
 LAST_CONTRACT = (((1,), (1,)), ((), ()))
-VMEM_LIMIT = 67043328
+SCORE_VMEM = 67043328
 
 UNITS = 2176
 HALF = 1088
@@ -33,7 +33,8 @@
 FIRST, SECOND, ONWARD = GATHER[:2], GATHER[2:4], GATHER[4:]
 DIM, FFN, COLS = 512, 2048, 256
 WEIGHT_SHAPES = ((2, DIM, FFN), (2, FFN, DIM), (DIM, DIM))
-COLOURS = ((0, 6, ('x', 'y', 'z')), (384, 6, ('y', 'z', 'x')), (768, 5, ('z', 'x', 'y')))
+COLOURS = ((0, 6), (384, 6), (768, 5))
+ORDERS = (('xyz', 'yzx', 'zxy'), ('zxy', 'xyz', 'yzx'))
 HANDS = ((LEFT, False), (RIGHT, False), (ACROSS, False), (ACROSS, True), (OWN, False))
 
 
@@ -144,20 +145,32 @@
     return dot(hidden, w_proj[...]).astype(BF16)
 
 
+def up_rows(ups):
+    return ups.at[pl.ds(0, 64)], ups.at[pl.ds(64, 128)]
+
+
+def arrivals(pairs, sems):
+    copies = [pltpu.make_async_copy(src, dst, sems.at[i]) for i, (src, dst) in enumerate(pairs)]
+    for c in copies:
+        c.start()
+    return copies
+
+
 def weight_loads(src, dst, sems, at=0):
     pairs = [(one.at[layer], two.at[layer]) for layer in range(2) for one, two in zip(src[:2], dst[:2])]
     return [pltpu.make_async_copy(one, two, sems.at[at + i]) for i, (one, two) in enumerate(pairs + [(src[2], dst[2])])]
 
 
 def score_kernel(
-    tau_ref, q_ref, d_ref, q_w1, q_w2, q_proj, d_w1, d_w2, d_proj, q_up, d_up, loss_ref,
-    q_all, d_all, st, stats, q_part, d_part, q_buf, d_buf, pair, loss_all, q_one, q_two, q_last, d_one, d_two, d_last, w_sems, *sems
+    tau_ref, q_ref, d_ref, q_w1, q_w2, q_proj, d_w1, d_w2, d_proj, ups, loss_ref,
+    q_all, d_all, st, stats, q_part, d_part, q_buf, d_buf, pair, loss_all, loss_row, q_one, q_two, q_last, d_one, d_two, d_last, w_sems, *sems
 ):
     q_weights, d_weights = (q_one, q_two, q_last), (d_one, d_two, d_last)
     q_loads = weight_loads((q_w1, q_w2, q_proj), q_weights, w_sems)
     d_loads = weight_loads((d_w1, d_w2, d_proj), d_weights, w_sems, len(q_loads))
     for c in q_loads + d_loads:
         c.start()
+    q_up, d_up = up_rows(ups)
     at = place()
     core, z = at['core'], at['z']
     other = moved(at, 'core', 1)
@@ -180,6 +193,15 @@
         here = d_all.at[core, pl.ds(docs_ring.spot[rel], 8)]
         return remote(here, here, sems, hands_at + rel, other)
 
+    used = [hands_at + SIDE + 1]
+
+    def broadcast(src, peers):
+        copies = [remote(src, src, sems, used[0] + i, p) for i, p in enumerate(peers)]
+        used[0] += len(peers)
+        for c in copies:
+            c.start()
+        return copies
+
     for h in range(2):
         def q_body(i, carry):
             def ready(step):
@@ -201,14 +223,14 @@
         rows = pl.ds(pl.multiple_of(i * 32, 32), 32)
         d_all[core, pl.ds(z * 8 + i * 2, 2)] = tower_forward(d_ref[rows, :], *d_weights, lambda step: None).reshape(2, 16, DIM)
 
-        @pl.when(i == 0)
-        def _():
-            for ring in q_thin:
-                ring.ag_pass()
-
         @pl.when(i == 1)
         def _():
             docs_ring.start(FIRST[:1] + SECOND[1:])
+            for ring in q_thin:
+                ring.ag_pass()
+
+        @pl.when(i == 2)
+        def _():
             for thin, wide in zip(q_thin, q_wide):
                 thin.take(SECOND + ONWARD)
                 wide.start(FIRST + SECOND)
@@ -218,9 +240,12 @@
     lax.fori_loop(0, SUB_COUNT, d_body, 0)
     docs_ring.start(FIRST[1:] + SECOND[:1])
     hand(OWN).start()
+    docs_ring.take(FIRST[:1])
+    docs_ring.start(ONWARD[:1])
     for ring in q_wide:
         ring.ag_pass()
-    docs_ring.ag_pass()
+    docs_ring.take(FIRST[1:])
+    docs_ring.start(ONWARD[1:])
     docs_ring.take(SECOND)
     hand(LEFT).start()
     hand(RIGHT).start()
@@ -233,61 +258,50 @@
 
     tau = tau_ref[0]
     queries = q_all[...].reshape(1024, DIM)
-    blocks = [(c, j) for c in range(2) for j in range(SIDE)]
-
-    def block(ref, c, j):
-        return ref[c, j * 8:(j + 1) * 8].reshape(128, DIM)
-
+    docs = d_all[...].reshape(1024, DIM)
     highs = []
-    for b, (c, j) in enumerate(blocks):
-        tile = dot(block(d_all, c, j), queries, LAST_CONTRACT) / tau
-        st[b] = tile
+    for b in range(SIDE):
+        rows = slice(b * COLS, (b + 1) * COLS)
+        tile = dot(docs[rows], queries, LAST_CONTRACT) / tau
+        st[rows] = tile
         highs.append(jnp.max(tile, axis=0, keepdims=True))
     high = functools.reduce(jnp.maximum, highs)
-    total = sum(jnp.sum(jnp.exp(st[b] - high), axis=0, keepdims=True) for b in range(len(blocks)))
+    blocks = [slice(b * 128, (b + 1) * 128) for b in range(8)]
+    total = sum(jnp.sum(jnp.exp(st[rows] - high), axis=0, keepdims=True) for rows in blocks)
+    stats[q_slot] = high + jnp.log(total)
+    shares = broadcast(stats.at[q_slot], q_peers)
+    for c in shares:
+        c.wait_recv()
+    all_stats = [stats[j] for j in range(16)]
+    top = functools.reduce(jnp.maximum, all_stats)
+    log_norm = top + jnp.log(sum(jnp.exp(part - top) for part in all_stats))
 
     def matches(rows):
         row = lax.broadcasted_iota(jnp.int32, (rows, 1024), 0)
         column = lax.broadcasted_iota(jnp.int32, (rows, 1024), 1)
         return (row < 64) & (column == jnp.where(row < 32, own[0] * 16 + row, 480 + own[1] * 16 + row))
 
-    positive = jnp.sum(jnp.where(matches(64), st[d_slot, 0:64, :], 0.0), axis=0, keepdims=True)
-    for i, row in enumerate((high, total, positive)):
-        stats[q_slot, i:i + 1, :] = row
-    extra = hands_at + SIDE
-    shares = [remote(stats.at[q_slot], stats.at[q_slot], sems, extra + i, p) for i, p in enumerate(q_peers)]
-    for c in shares:
-        c.start()
-    for c in shares:
-        c.wait_recv()
-    all_stats = [stats[j] for j in range(16)]
-    top = functools.reduce(jnp.maximum, [s[0:1] for s in all_stats])
-    norm = sum(s[1:2] * jnp.exp(s[0:1] - top) for s in all_stats)
-    log_norm = top + jnp.log(norm)
-    part = jnp.sum(log_norm - sum(s[2:3] for s in all_stats), axis=1, keepdims=True)
-    loss_all[d_slot] = jnp.broadcast_to(part, (8, 128))
-    extra = extra + len(shares)
-    losses = [remote(loss_all.at[d_slot], loss_all.at[d_slot], sems, extra + i, p) for i, p in enumerate(d_peers)]
-    for c in losses:
-        c.start()
+    def spread(values):
+        return jnp.broadcast_to(jnp.sum(values, keepdims=True), (1, 128))
+
+    positive = st[pl.ds(pl.multiple_of(d_slot * 128, 128), 64), :]
+    loss_all[d_slot] = spread(jnp.where(matches(64), log_norm - positive, 0.0))
+    losses = broadcast(loss_all.at[d_slot], d_peers)
 
     scale = 8192.0 * tau
     hit = matches(128)
     grads = []
-    for b in range(len(blocks)):
-        soft = jnp.exp(st[b] - log_norm) - jnp.where(hit & (d_slot == b), 1.0, 0.0)
+    for b, rows in enumerate(blocks):
+        soft = jnp.exp(st[rows] - log_norm) - jnp.where(hit & (d_slot == b), 1.0, 0.0)
         grads.append((soft / scale).astype(BF16))
     grad = jnp.concatenate(grads, axis=0)
-    docs = d_all[...].reshape(1024, DIM)
     q_wide, q_thin = zip(*[q_rings(q_part, h) for h in range(2)])
     for h in range(2):
         q_part[h] = dot(grad[:, h * DIM:(h + 1) * DIM], docs, ROWS_CONTRACT).reshape(32, 16, DIM)
         q_wide[h].start(FAR + NEAR)
-
-    extra = extra + len(losses)
-    for b, (c, j) in enumerate(blocks):
-        d_part[c, j * 8:(j + 1) * 8] = dot(grads[b], queries).reshape(8, 16, DIM)
-    swap = remote(d_part.at[other['core']], pair, sems, extra, other)
+    for c in range(2):
+        d_part[c] = dot(grad[c * DIM:(c + 1) * DIM], queries).reshape(32, 16, DIM)
+    swap = remote(d_part.at[other['core']], pair, sems, hands_at + SIDE, other)
     swap.start()
     docs_sum = Ring(at, 'z', d_part.at[core], 0, 8, d_buf, 0, sems, 4)
     q_wide[0].rs_pass()
@@ -299,17 +313,21 @@
         wide.rs_end()
         thin.start(FAR + NEAR)
     docs_sum.rs_pass()
+    for c in losses:
+        c.wait_recv()
+    loss_row[q_slot] = sum(loss_all[j] for j in range(8))
+    row_losses = broadcast(loss_row.at[q_slot], q_peers)
     for ring in q_thin:
         ring.rs_pass()
-    for c in losses:
-        c.wait_recv()
-    loss_ref[...] = sum(loss_all[j, 0:1, 0:1] for j in range(8)) / 8192.0
     for h, ring in enumerate(q_thin):
         ring.rs_end()
         q_up[h * 32:(h + 1) * 32, :] = q_part[h, pl.ds(own[h], 2)].reshape(32, DIM).astype(BF16)
     docs_sum.rs_end()
+    for c in row_losses:
+        c.wait_recv()
+    loss_ref[...] = sum(loss_row[j, :, 0:1] for j in range(16)) / 8192.0
     d_up[...] = d_part[core, pl.ds(z * 8, 8)].reshape(128, DIM).astype(BF16)
-    for c in shares + losses + [swap] + list(map(hand, range(SIDE))):
+    for c in shares + losses + row_losses + [swap] + list(map(hand, range(SIDE))):
         c.wait_send()
     for ring in (*q_wide, *q_thin, docs_sum):
         ring.sent(FAR + NEAR + ON)
@@ -321,29 +339,30 @@
 
 def scores(tau, q_rows, d_rows, weights):
     vmem, whole = pl.BlockSpec(memory_space=pltpu.VMEM), pl.BlockSpec(memory_space=pl.ANY)
-    copies = 5 * len(MESSAGES) + 27
+    copies = 5 * len(MESSAGES) + 42
     return pl.pallas_call(
         score_kernel,
-        out_shape=tuple(jax.ShapeDtypeStruct(*s) for s in (((64, DIM), BF16), ((128, DIM), BF16), ((1, 1), F32))),
+        out_shape=(jax.ShapeDtypeStruct((192, DIM), BF16), jax.ShapeDtypeStruct((1, 1), F32)),
         in_specs=[pl.BlockSpec(memory_space=pltpu.SMEM), vmem, vmem] + [whole] * 6,
-        out_specs=(vmem,) * 3,
+        out_specs=(vmem,) * 2,
         scratch_shapes=[
             pltpu.VMEM((2, 32, 16, DIM), BF16),
             pltpu.VMEM((2, 32, 16, DIM), BF16),
-            pltpu.VMEM((8, 128, 1024), F32),
-            pltpu.VMEM((16, 3, 1024), F32),
+            pltpu.VMEM((1024, 1024), F32),
+            pltpu.VMEM((16, 1, 1024), F32),
             pltpu.VMEM((2, 32, 16, DIM), F32),
             pltpu.VMEM((2, 32, 16, DIM), F32),
             pltpu.VMEM((2, 30, 16, DIM), F32),
             pltpu.VMEM((24, 16, DIM), F32),
             pltpu.VMEM((32, 16, DIM), F32),
-            pltpu.VMEM((8, 8, 128), F32),
+            pltpu.VMEM((8, 1, 128), F32),
+            pltpu.VMEM((16, 1, 128), F32),
             *[pltpu.VMEM(shape, BF16) for shape in WEIGHT_SHAPES * 2],
             pltpu.SemaphoreType.DMA((10,)),
             pltpu.SemaphoreType.DMA((copies,)),
             pltpu.SemaphoreType.DMA((copies,)),
         ],
-        compiler_params=pltpu.CompilerParams(collective_id=0, has_side_effects=True, vmem_limit_bytes=VMEM_LIMIT),
+        compiler_params=pltpu.CompilerParams(collective_id=0, has_side_effects=True, vmem_limit_bytes=SCORE_VMEM),
         name='towers_forward_scores',
     )(tau, q_rows, d_rows, *weights)
 
@@ -352,17 +371,20 @@
     return jax.vjp(jax.nn.gelu, pre)[1](act_grad)[0]
 
 
-def tower_backward(sub, rows_per, x_ref, up_ref, w_one, w_two, w_proj, acc, pre_s, act_s, hook):
-    rows = pl.ds(pl.multiple_of(sub * rows_per, rows_per), rows_per)
+def tower_backward(sub, rows_per, x_ref, up_ref, w_one, w_two, w_proj, acc, pre_s, act_s, hook, ready=None):
+    first = ready is not None
+    rows = pl.ds(0 if first else pl.multiple_of(sub * rows_per, rows_per), rows_per)
+    ready = ready or (lambda step: None)
     hidden = [x_ref[rows, :]]
     for layer in range(2):
+        ready(2 * layer)
         pre = dot(hidden[layer], w_one[layer])
         pre_s[layer, 0:rows_per] = pre
         act = jax.nn.gelu(pre).astype(BF16)
         act_s[layer, 0:rows_per] = act
-        if layer == 0:
-            hook(0)
+        ready(2 * layer + 1)
         hidden.append((hidden[layer].astype(F32) + dot(act, w_two[layer])).astype(BF16))
+    ready(4)
     hook(1)
     up = up_ref[rows, :]
 
@@ -371,7 +393,8 @@
             part = dot(lhs[:, i * COLS:(i + 1) * COLS], rhs, ROWS_CONTRACT)
             for j in range(2):
                 spot = base + j * stride + i * 32
-                acc[spot:spot + 32] += part[:, j * COLS:(j + 1) * COLS].reshape(32, 8, COLS)
+                tile = part[:, j * COLS:(j + 1) * COLS].reshape(32, 8, COLS)
+                acc[spot:spot + 32] = tile if first else acc[spot:spot + 32] + tile
 
     add(FFN, 64, hidden[2], up)
     resid = dot(up, w_proj[...], LAST_CONTRACT)
@@ -399,7 +422,8 @@
         greet([self.other] + self.around)
         self.rings = {}
         for t in (Q, D):
-            for k, (first, rows, dims) in enumerate(COLOURS):
+            for k, (first, rows) in enumerate(COLOURS):
+                dims = ORDERS[t][k]
                 base = self.core * HALF + first
                 for p in (OUTER, MIDDLE, INNER):
                     n = rows * RING_SIZE[p]
@@ -493,8 +517,10 @@
             self.hand(*h).wait_send()
 
 
-def train_kernel(q_in, d_in, q_up, d_up, q_w1, q_w2, q_proj, d_w1, d_w2, d_proj, acc, w_one, w_two, w_proj, pre_s, act_s, pair, *rest):
+def train_kernel(q_hbm, d_hbm, ups_hbm, q_w1, q_w2, q_proj, d_w1, d_w2, d_proj, acc, w_one, w_two, w_proj, pre_s, act_s, pair, q_in, d_in, ups, in_sems, *rest):
+    q_up, d_up = up_rows(ups)
     bufs, w_sems, sems = rest[:3], rest[3], rest[4:]
+    loads = arrivals(((q_hbm, q_in), (d_hbm, d_in), (ups_hbm, ups)), in_sems)
     ex = Exchange(acc, pair, bufs, sems)
 
     held = (w_one, w_two, w_proj)
@@ -502,20 +528,14 @@
     for c in q_loads:
         c.start()
 
-    def clear(i, carry):
-        for t in (Q, D):
-            acc[t, pl.ds(i * 16, 16)] = jnp.zeros((16, 8, COLS), F32)
-        return carry
-
-    lax.fori_loop(0, UNITS // 16, clear, 0)
-    for c in q_loads:
-        c.wait()
-
     def at_hooks(sub, table):
         def hook(i):
             for when, work in table:
                 if when[1] == i:
-                    pl.when(sub == when[0])(work)
+                    if isinstance(sub, int):
+                        work() if sub == when[0] else None
+                    else:
+                        pl.when(sub == when[0])(work)
 
         return hook
 
@@ -531,15 +551,14 @@
         tower_backward(sub, 16, q_in, q_up, *held, acc.at[Q], pre_s, act_s, hook)
         return carry
 
-    lax.fori_loop(0, SUB_COUNT, q_body, 0)
+    for c in loads:
+        c.wait()
+    tower_backward(0, 16, q_in, q_up, *held, acc.at[Q], pre_s, act_s, lambda i: None, lambda step: q_loads[step].wait())
+    lax.fori_loop(1, SUB_COUNT, q_body, 0)
     d_loads[1].start()
     ex.met()
     ex.pairs(Q, ACROSS, fresh=True)
     ex.pairs(Q, RIGHT, fresh=True)
-    d_loads[0].wait()
-    for c in d_loads[2:]:
-        c.wait()
-
     def across():
         ex.settle(Q, ACROSS)
         ex.start(Q, OUTER, FAR)
@@ -557,7 +576,7 @@
         ex.rs_pass(Q, OUTER)
 
     steps = (
-        ((0, 0), d_loads[1].wait), ((0, 2), across), ((0, 3), right),
+        ((0, 2), across), ((0, 3), right),
         ((1, 1), functools.partial(ex.pairs, Q, OWN)), ((1, 2), left), ((1, 3), own),
     )
 
@@ -565,7 +584,8 @@
         tower_backward(sub, 32, d_in, d_up, *held, acc.at[D], pre_s, act_s, at_hooks(sub, steps))
         return carry
 
-    lax.fori_loop(0, SUB_COUNT, d_body, 0)
+    tower_backward(0, 32, d_in, d_up, *held, acc.at[D], pre_s, act_s, at_hooks(0, steps), lambda step: d_loads[step].wait())
+    lax.fori_loop(1, SUB_COUNT, d_body, 0)
     ex.pairs(D, ACROSS)
     ex.pairs(D, RIGHT)
     ex.rs_end(Q, OUTER)
@@ -619,27 +639,31 @@
     ex.finish()
 
 
-def train(q_rows, d_rows, q_up, d_up, weights):
+def train(q_rows, d_rows, ups, weights):
     vmem, whole = pl.BlockSpec(memory_space=pltpu.VMEM), pl.BlockSpec(memory_space=pl.ANY)
     bufs = [pltpu.VMEM((3 * HALF // SIDE ** p // SIDE, 8, COLS), F32) for p in (OUTER, MIDDLE, INNER)]
     dma = pltpu.SemaphoreType.DMA
     return pl.pallas_call(
         train_kernel,
         out_shape=pltpu.VMEM((2, UNITS, 8, COLS), F32),
-        in_specs=[vmem] * 4 + [whole] * 6,
+        in_specs=[whole] * 9,
         out_specs=vmem,
         scratch_shapes=[
             *[pltpu.VMEM(shape, BF16) for shape in WEIGHT_SHAPES],
             pltpu.VMEM((2, 32, FFN), F32),
             pltpu.VMEM((2, 32, FFN), BF16),
             pltpu.VMEM((2, 272, 8, COLS), F32),
+            pltpu.VMEM(q_rows.shape, BF16),
+            pltpu.VMEM(d_rows.shape, BF16),
+            pltpu.VMEM(ups.shape, BF16),
+            pltpu.SemaphoreType.DMA((3,)),
             *bufs,
             dma((5,)), *[dma((n,)) for n in (24, 24, 216, 216, 90, 90)],
             pltpu.SemaphoreType.REGULAR((2,)), pltpu.SemaphoreType.REGULAR((8,)),
         ],
         compiler_params=pltpu.CompilerParams(collective_id=1, has_side_effects=True, vmem_limit_bytes=TRAIN_VMEM),
         name='towers_backward_all_reduce',
-    )(q_rows, d_rows, q_up, d_up, *weights)
+    )(q_rows, d_rows, ups, *weights)
 
 
 def unpack_kernel(acc, *rest):
@@ -677,8 +701,8 @@
 
 def local_step(q_loc, d_loc, temperature, *weights):
     d_rows = d_loc.reshape(-1, d_loc.shape[-1])
-    q_up, d_up, loss = scores(temperature.reshape(1), q_loc, d_rows, weights)
-    return (loss.reshape(()), *unpack(train(q_loc, d_rows, q_up, d_up, weights)))
+    ups, loss = scores(temperature.reshape(1), q_loc, d_rows, weights)
+    return (loss.reshape(()), *unpack(train(q_loc, d_rows, ups, weights)))
 
 
 def solution(mesh):

time: 261 us -> 255 us (0.977)
  Pallas kernels: 258 us -> 252 us
    pallas_call x1, Pallas kernels: 62.2 us -> 57.8 us  [scores(): pl.pallas_call(score_kernel, out_shape=(jax.ShapeDtypeStruct((192, DIM),...]
where the time goes in v4:
time: 255 us
  Pallas kernels  252 us (99%)
  between operations  2.99 us (1%)
    pallas_call x1, Pallas kernels, train(): pl.pallas_call(train_kernel, out_shape=pltpu.VMEM((2, UNITS, 8, COLS), F3...  182 us
    pallas_call x1, Pallas kernels, scores(): pl.pallas_call(score_kernel, out_shape=(jax.ShapeDtypeStruct((192, DIM),...  57.8 us
    pallas_call x1, Pallas kernels, unpack(): pl.pallas_call(unpack_kernel, out_shape=tuple((jax.ShapeDtypeStruct(s, F3...  11.9 us

profile of v4, /device:TPU:1, one launch (start us, length us, event | category | flops | bytes accessed | tf_op | source)
XLA Modules:
  0.0 255.1 jit_solution(15539204161146176143)
XLA Ops:
  1.3 57.8 %towers_forward_scores.1 = (bf16[192,512]{1,0:T(8,128)(2,1)}, f32[1,1]{1,0:T(1,128)}) custom-call(f32[1]{0:T(128)} %bitcast.9.tau_ref, bf16[64,512]{1,0:T(8,128)(2,1)} %q_hbm.1, bf16[128,512]{1,0:T(8,128)(2,1)} %bitcast.10, bf16[2,512,2048]{2,1,0:T(8,128)(2,1)} %q_w1.3, bf16[2,2048,512]{2,1,0:T(8,128)(2,1)} %q_w2.3, bf16[512,512]{1,0:T(8,128)(2,1)} %q_proj.3, ...), custom_call_target="tpu_custom_call" | custom-call | tf_op jit(solution)/shard_map/towers_forward_scores/pallas_call | solution.py:343
  59.1 182.4 %towers_backward_all_reduce.1.acc = f32[2,2176,8,256]{3,2,1,0:T(8,128)S(1)} custom-call(bf16[64,512]{1,0:T(8,128)(2,1)} %q_hbm.1, bf16[128,512]{1,0:T(8,128)(2,1)} %bitcast.11, bf16[192,512]{1,0:T(8,128)(2,1)} %get-tuple-element.16.ups_hbm, bf16[2,512,2048]{2,1,0:T(8,128)(2,1)} %q_w1.3, bf16[2,2048,512]{2,1,0:T(8,128)(2,1)} %q_w2.3, ...), custom_call_target="tpu_custom_call" | custom-call | tf_op jit(solution)/shard_map/towers_backward_all_reduce/pallas_call | solution.py:646
  241.5 11.9 %unpack.1 = (f32[2,64,8,2048]{3,2,1,0:T(8,128)}, f32[2,256,8,512]{3,2,1,0:T(8,128)}, f32[64,8,512]{2,1,0:T(8,128)}, f32[2,64,8,2048]{3,2,1,0:T(8,128)}, f32[2,25...) custom-call(f32[2,2176,8,256]{3,2,1,0:T(8,128)S(1)} %towers_backward_all_reduce.1.acc), custom_call_target="tpu_custom_call" | custom-call | tf_op jit(solution)/shard_map/unpack/pallas_call | solution.py:690

commit v5 on v4

--- a/solution.py
+++ b/solution.py
@@ -260,8 +260,8 @@
     queries = q_all[...].reshape(1024, DIM)
     docs = d_all[...].reshape(1024, DIM)
     highs = []
-    for b in range(SIDE):
-        rows = slice(b * COLS, (b + 1) * COLS)
+    for b in range(2):
+        rows = slice(b * DIM, (b + 1) * DIM)
         tile = dot(docs[rows], queries, LAST_CONTRACT) / tau
         st[rows] = tile
         highs.append(jnp.max(tile, axis=0, keepdims=True))

time: 255 us -> 255 us (level)
  no operation moved by 1% of the time
where the time goes in v5:
time: 255 us
  Pallas kernels  252 us (99%)
  between operations  2.99 us (1%)
    pallas_call x1, Pallas kernels, train(): pl.pallas_call(train_kernel, out_shape=pltpu.VMEM((2, UNITS, 8, COLS), F3...  183 us
    pallas_call x1, Pallas kernels, scores(): pl.pallas_call(score_kernel, out_shape=(jax.ShapeDtypeStruct((192, DIM),...  57.7 us
    pallas_call x1, Pallas kernels, unpack(): pl.pallas_call(unpack_kernel, out_shape=tuple((jax.ShapeDtypeStruct(s, F3...  11.9 us

profile of v5, /device:TPU:1, one launch (start us, length us, event | category | flops | bytes accessed | tf_op | source)
XLA Modules:
  0.0 255.1 jit_solution(8274390679830201553)
XLA Ops:
  1.3 57.7 %towers_forward_scores.1 = (bf16[192,512]{1,0:T(8,128)(2,1)}, f32[1,1]{1,0:T(1,128)}) custom-call(f32[1]{0:T(128)} %bitcast.9.tau_ref, bf16[64,512]{1,0:T(8,128)(2,1)} %q_hbm.1, bf16[128,512]{1,0:T(8,128)(2,1)} %bitcast.10, bf16[2,512,2048]{2,1,0:T(8,128)(2,1)} %q_w1.3, bf16[2,2048,512]{2,1,0:T(8,128)(2,1)} %q_w2.3, bf16[512,512]{1,0:T(8,128)(2,1)} %q_proj.3, ...), custom_call_target="tpu_custom_call" | custom-call | tf_op jit(solution)/shard_map/towers_forward_scores/pallas_call | solution.py:343
  59.0 182.5 %towers_backward_all_reduce.1.acc = f32[2,2176,8,256]{3,2,1,0:T(8,128)S(1)} custom-call(bf16[64,512]{1,0:T(8,128)(2,1)} %q_hbm.1, bf16[128,512]{1,0:T(8,128)(2,1)} %bitcast.11, bf16[192,512]{1,0:T(8,128)(2,1)} %get-tuple-element.16.ups_hbm, bf16[2,512,2048]{2,1,0:T(8,128)(2,1)} %q_w1.3, bf16[2,2048,512]{2,1,0:T(8,128)(2,1)} %q_w2.3, ...), custom_call_target="tpu_custom_call" | custom-call | tf_op jit(solution)/shard_map/towers_backward_all_reduce/pallas_call | solution.py:646
  241.5 11.9 %unpack.1 = (f32[2,64,8,2048]{3,2,1,0:T(8,128)}, f32[2,256,8,512]{3,2,1,0:T(8,128)}, f32[64,8,512]{2,1,0:T(8,128)}, f32[2,64,8,2048]{3,2,1,0:T(8,128)}, f32[2,25...) custom-call(f32[2,2176,8,256]{3,2,1,0:T(8,128)S(1)} %towers_backward_all_reduce.1.acc), custom_call_target="tpu_custom_call" | custom-call | tf_op jit(solution)/shard_map/unpack/pallas_call | solution.py:690
